TPU v7x, 256 devices: a 8x8x2 block of a 8x8x16 slice. The times are simulated.
256 devices in a mesh: groups: 2 (over z), ep: 16 (over x, core), tp: 8 (over y).
Axes of the slice: x: 8, y: 8, z: 2, core: 2. Of those that a mesh axis runs over, the one named last changes fastest.
The devices are a block of a 8x8x16 slice.
Arguments:
- tokens: bfloat16 [1024, 7168], P(('groups', 'ep')), parts along dimension 0, may hold values from -6 to 6
- w_gate: bfloat16 [16, 7168, 2048], P('ep', None, 'tp'), may hold values from -0.0625 to 0.0625
- w_up: bfloat16 [16, 7168, 2048], P('ep', None, 'tp'), may hold values from -0.0625 to 0.0625
- w_down: bfloat16 [16, 2048, 7168], P('ep', 'tp'), may hold values from -0.1875 to 0.1875
- router_logits: float32 [1024, 8], P(('groups', 'ep')), parts along dimension 0, may hold values from -6 to 6
- expert_ids: int32 [1024, 8], P(('groups', 'ep')), parts along dimension 0, may hold values from 0 to 15, all different within a row; in each aligned block of 32 rows (0 to 31, 32 to 63, ...) at most 24 rows name the same one
- draft_lengths: int32 [128], P(('groups', 'ep')), parts along dimension 0, may hold values from 7 to 8
- accept_mask: int32 [128, 8], P(('groups', 'ep')), parts along dimension 0, may hold values 0 or 1
Outputs:
- mixed: bfloat16 [1024, 7168], P(('groups', 'ep'), 'tp'), parts along dimension 0
- accepted: int32 [2], P('groups'), parts along dimension 0
There are 2 independent parts, one for each index of `groups`. A program takes and returns all parts, laid end to end along the dimension named above; an argument that names none is the same for every part. Nothing has to cross between parts.
Inputs may be any that keep to these rules, and one draw needn't show every extreme that they name: `expert_ids`: each row names 8 different experts. Among the rows of one ep index (aligned blocks of 32 rows) no expert is named by more than 24 rows, and in every draw some expert is named by exactly 24 rows of some block.
All inputs are finite; a program needn't handle non-finite values. No bound on the sum of `accept_mask` on one device may be relied on, other than what follows from the above.
Results may differ from a plain program's by a relative error of at most 0.017.
Values may be sent and summed in bfloat16 or wider, within the bound.
A program may use at most 128 MiB of HBM per device.

v0:
```python
import jax
import jax.numpy as jnp
from jax import lax
from jax.sharding import PartitionSpec as P

DRAFT = 8
EXPERTS = 16
CAP = 24


def sent_to_all(array, axis):
    copies = jnp.broadcast_to(array, (lax.axis_size(axis), *array.shape))
    return lax.all_to_all(copies, axis, split_axis=0, concat_axis=0, tiled=True)


def of_everyone(array, axis):
    everything = sent_to_all(array, axis)
    return jnp.sum(everything, axis=0)


def per_device(tokens, w_gate, w_up, w_down, router_logits, expert_ids, draft_lengths, accept_mask):
    tok_rows = tokens.shape[0]
    width = tokens.shape[1]
    top = expert_ids.shape[1]
    tp_count = lax.axis_size("tp")
    slice_width = width // tp_count
    live = jnp.arange(DRAFT, dtype=jnp.int32)[None, :] < draft_lengths[:, None]
    live_rows = live.reshape(tok_rows)
    live_tokens = jnp.where(live_rows[:, None], tokens, jnp.zeros((), tokens.dtype))
    sig = jax.nn.sigmoid(router_logits)
    gates = 2.827 * sig / jnp.sum(sig, axis=1, keepdims=True)
    flat_ids = expert_ids.reshape(-1)
    onehot = (flat_ids[:, None] == jnp.arange(EXPERTS, dtype=jnp.int32)[None, :]).astype(jnp.int32)
    rank = jnp.cumsum(onehot, axis=0) - 1
    slot = jnp.sum(rank * onehot, axis=1)
    target = flat_ids * CAP + slot
    source = jnp.arange(tok_rows * top, dtype=jnp.int32) // top
    own_cols = lax.dynamic_slice_in_dim(
        live_tokens, lax.axis_index("tp") * slice_width, slice_width, 1
    )
    sendbuf = jnp.zeros((EXPERTS * CAP, slice_width), tokens.dtype).at[target].set(own_cols[source])
    received = lax.all_to_all(
        sendbuf.reshape(EXPERTS, CAP, slice_width), "ep", split_axis=0, concat_axis=1, tiled=True
    )
    piece = lax.all_gather(received, "tp", axis=2, tiled=True)
    gate_sum = jnp.einsum("emd,edf->emf", piece, w_gate, preferred_element_type=jnp.float32)
    up_sum = jnp.einsum("emd,edf->emf", piece, w_up, preferred_element_type=jnp.float32)
    hidden = (jax.nn.silu(gate_sum) * up_sum).astype(jnp.bfloat16)
    partial_value = jnp.einsum("emf,efd->emd", hidden, w_down, preferred_element_type=jnp.float32)
    expert_out = lax.psum_scatter(
        partial_value.astype(jnp.bfloat16), "tp", scatter_dimension=2, tiled=True
    )
    returned = lax.all_to_all(expert_out, "ep", split_axis=1, concat_axis=0, tiled=True)
    flat_back = returned.reshape(EXPERTS * CAP, returned.shape[2])
    picked = flat_back[target].reshape(tok_rows, top, returned.shape[2])
    mixed = jnp.sum(gates[:, :, None] * picked.astype(jnp.float32), axis=1).astype(jnp.bfloat16)
    passed = accept_mask * live.astype(jnp.int32)
    prefix = jnp.cumprod(passed, axis=1)
    local_count = jnp.sum(prefix)
    total = of_everyone(local_count, "ep")
    accepted = total.reshape(1)
    return (mixed, accepted)


def solution(mesh):
    placed = (
        P(("groups", "ep"), None),
        P("ep", None, "tp"),
        P("ep", None, "tp"),
        P("ep", "tp", None),
        P(("groups", "ep"), None),
        P(("groups", "ep"), None),
        P(("groups", "ep")),
        P(("groups", "ep"), None),
    )
    return jax.shard_map(
        per_device,
        mesh=mesh,
        in_specs=placed,
        out_specs=(P(("groups", "ep"), "tp"), P("groups")),
        check_vma=False,
    )
```

profile of v0, /device:TPU:516, one launch (start us, length us, event | category | flops | bytes accessed | tf_op | source)
XLA Modules:
  0.0 282.5 jit_solution(15594155464627464665)
XLA Ops:
  7.2 0.1 all-gather.2.cloned.1.call-start
  7.2 0.8 copy.36
  8.0 0.1 eq.29
  8.1 0.1 eq.25
  8.2 0.7 broadcast_multiply_fusion
  8.9 0.6 reduce-window.6
  9.5 0.2 slice_reduce_fusion
  9.7 0.1 copy.35
  9.8 0.1 mul.55
  9.9 0.7 iota_compare_fusion.2
  10.6 0.1 lt.48
  10.7 0.1 fusion.23
  10.8 0.9 dynamic-slice_select_fusion
  11.7 3.5 %scatter_custom_fusion = bf16[384,896]{1,0:T(8,128)(2,1)S(1)} fusion(s32[256]{0:T(256)S(1)} %bitcast.67, bf16[32,896]{1,0:T(8,128)(2,1)S(1)} %dynamic-slice_select_fusion, s32[1024]{0:T(1024)S(1)} %pad_clamp_fusion.1, bf16[]{:T(256)} %constant.43.clone.1), kind=kCustom, calls=%fused_computation.19 | custom fusion | bytes 688130 | tf_op jit(solution)/shard_map/scatter | solution.py:41
  15.2 41.2 %all_to_all.27 = bf16[16,24,896]{2,1,0:T(8,128)(2,1)} all-to-all(bf16[16,24,896]{2,1,0:T(8,128)(2,1)S(1)} %bitcast.66), channel_id=1, replica_groups=mesh['groups'=2,'ep'=16,'tp'=8] {'ep'}, dimensions={0} | all-to-all | bytes 1376256 | tf_op jit(solution)/shard_map/all_to_all | solution.py:42
  56.4 0.1 all-gather.2.cloned.1.call-update
  56.4 0.1 reduce-scatter.4.cloned.1.call-start
  56.5 68.7 %all-gather.2.cloned.1.call-done = bf16[1,384,7168]{2,1,0:T(8,128)(2,1)} async-done(((bf16[1,384,896]{2,1,0:T(8,128)(2,1)}), bf16[1,384,7168]{2,1,0:T(8,128)(2,1)}) %all-gather.2.cloned.1.call-update) | async-done | bytes 5505040 | tf_op jit(solution)/shard_map/all_gather | solution.py:45
  125.2 5.4 %fusion.3 = f32[384,256]{1,0:T(8,128)S(1)} fusion(bf16[1,384,7168]{2,1,0:T(8,128)(2,1)} %all-gather.2.cloned.1.call-done, bf16[1,7168,256]{2,1,0:T(8,128)(2,1)} %param.9), kind=kOutput, calls=%fused_computation.8 | convolution fusion | flops 1409286144 | bytes 9568256 | tf_op jit(solution)/shard_map/emd,edf->emf/dot_general | solution.py:46
  130.6 0.9 copy-done.5
  131.5 1.6 fusion.13
  133.1 0.4 copy-done
  133.5 4.0 %fusion = bf16[1,384,7168]{2,1,0:T(8,128)(2,1)} fusion(bf16[384,256]{1,0:T(8,128)(2,1)S(1)} %fusion.13, bf16[1,256,7168]{2,1,0:T(8,128)(2,1)S(1)} %copy-done), kind=kOutput, calls=%fused_computation.4 | convolution fusion | flops 1412038656 | bytes 9371648 | tf_op jit(solution)/shard_map/emf,efd->emd/dot_general | solution.py:49
  137.5 24.0 %copy.41 = bf16[1,384,7168]{1,0,2:T(2,128)(2,1)} copy(bf16[1,384,7168]{2,1,0:T(8,128)(2,1)} %fusion) | data formatting | bytes 11010048
  161.5 7.4 %copy.51 = bf16[7168,1,384]{2,0,1:T(8,128)(2,1)} copy(bf16[7168,1,384]{2,1,0:T(2,128)(2,1)} %bitcast.60) | data formatting | bytes 11010048
  168.9 0.1 reduce-scatter.4.cloned.1.call-update
  169.0 0.6 copy-done.2
  169.6 0.1 broadcast_select_fusion
  169.7 0.2 reduce_window.9
  169.9 0.6 reduce_sum.51
  170.5 1.2 broadcast_in_dim.29
  171.8 7.3 %all-to-all-start.2 = ((s32[16,1,1]{2,1,0:T(1,128)}), s32[16,1,1]{2,1,0:T(1,128)S(1)}, u32[]{:S(2)}, u32[]{:S(2)}) async-start(s32[16,1,1]{2,1,0:T(1,128)} %broadcast_in_dim.29), calls=%async_computation.2 | async-start | bytes 16384 | tf_op jit(solution)/shard_map/all_to_all | solution.py:13
  179.0 58.0 %reduce-scatter.4.cloned.1.call-done = bf16[896,384]{1,0:T(8,128)(2,1)} async-done(((bf16[7168,384]{1,0:T(8,128)(2,1)}), bf16[896,384]{1,0:T(8,128)(2,1)}) %reduce-scatter.4.cloned.1.call-update) | async-done | bytes 688144
  237.0 1.8 reshape_bitcast_fusion
  238.8 0.0 copy-start.1
  238.8 2.3 copy.39
  241.1 0.5 broadcast.160
  241.6 4.8 %reduce.3 = bf16[384,896]{1,0:T(8,128)(2,1)S(1)} reduce(bf16[384,1,896]{2,1,0:T(2,128)(2,1)S(1)} %bitcast.63, bf16[]{:T(256)} %broadcast.160), dimensions={1}, to_apply=%bitcast.54.reduce_sub_computation | reduce | bytes 1376258
  246.5 1.0 reshape.202
  247.5 0.0 all-to-all-done.2
  247.5 7.3 %all-to-all-start.1 = ((bf16[16,2,10752]{2,1,0:T(2,128)(2,1)}), bf16[16,2,10752]{2,1,0:T(2,128)(2,1)S(1)}, u32[]{:S(2)}, u32[]{:S(2)}) async-start(bf16[16,2,10752]{2,1,0:T(2,128)(2,1)} %reshape.202), calls=%async_computation.1 | async-start | bytes 1376256 | tf_op jit(solution)/shard_map/all_to_all | solution.py:53
  254.8 0.1 copy.34
  254.9 0.7 reduce_sum.52
  255.6 17.3 %all-to-all-done.1 = bf16[16,2,10752]{2,1,0:T(2,128)(2,1)S(1)} async-done(((bf16[16,2,10752]{2,1,0:T(2,128)(2,1)}), bf16[16,2,10752]{2,1,0:T(2,128)(2,1)S(1)}, u32[]{:S(2)}, u32[]{:S(2)}) %all-to-all-start.1) | async-done | bytes 688160 | tf_op jit(solution)/shard_map/all_to_all | solution.py:53
  272.8 0.6 reshape.203
  273.4 0.1 copy.52
  273.5 1.2 gather_fusion
  274.7 1.0 fusion.18
  (17 shorter events, 0.1 us)
Async XLA Ops:
  7.2 118.0 %all-gather.2.cloned.1.call-start = ((), (), s32[]{:S(2)}) async-start(), calls=%async_computation.4 | async-start | bytes 6193152 | tf_op jit(solution)/shard_map/all_gather | solution.py:45
  56.4 180.5 %reduce-scatter.4.cloned.1.call-start = ((), (), s32[]{:S(2)}) async-start(), calls=%async_computation.5 | async-start | bytes 6193152
  125.2 5.4 %copy-start.4 = (bf16[1,384,7168]{2,1,0:T(8,128)(2,1)S(1)}, bf16[1,384,7168]{2,1,0:T(8,128)(2,1)}, u32[]{:S(2)}) copy-start(bf16[1,384,7168]{2,1,0:T(8,128)(2,1)} %all-gather.2.cloned.1.call-done) | copy-start | bytes 16515076
  125.2 6.3 %copy-start.5 = (bf16[1,7168,256]{2,1,0:T(8,128)(2,1)S(1)}, bf16[1,7168,256]{2,1,0:T(8,128)(2,1)}, u32[]{:S(2)}) copy-start(bf16[1,7168,256]{2,1,0:T(8,128)(2,1)} %param.10) | copy-start | bytes 11010052
  131.5 2.0 copy-start
  168.9 0.7 copy-start.2
  168.9 0.7 copy-start.3
  171.8 75.8 %all-to-all-start.2 = ((s32[16,1,1]{2,1,0:T(1,128)}), s32[16,1,1]{2,1,0:T(1,128)S(1)}, u32[]{:S(2)}, u32[]{:S(2)}) async-start(s32[16,1,1]{2,1,0:T(1,128)} %broadcast_in_dim.29), calls=%async_computation.2 | async-start | bytes 16384 | tf_op jit(solution)/shard_map/all_to_all | solution.py:13
  238.8 16.0 %copy-start.1 = (f32[32,8]{0,1:T(8,128)S(1)}, f32[32,8]{0,1:T(8,128)}, u32[]{:S(2)}) copy-start(f32[32,8]{0,1:T(8,128)} %param.12) | copy-start | bytes 3076
  247.5 25.3 %all-to-all-start.1 = ((bf16[16,2,10752]{2,1,0:T(2,128)(2,1)}), bf16[16,2,10752]{2,1,0:T(2,128)(2,1)S(1)}, u32[]{:S(2)}, u32[]{:S(2)}) async-start(bf16[16,2,10752]{2,1,0:T(2,128)(2,1)} %reshape.202), calls=%async_computation.1 | async-start | bytes 1376256 | tf_op jit(solution)/shard_map/all_to_all | solution.py:53
Sparse Core Ops, SparseCore 0:
  56.5 68.5 all-gather.1
  169.1 67.8 reduce-scatter.3
where the time goes:
time: 288 us; the launch traced here: 283 us
  waiting for transfers between devices  144 us (50%)
  local copies, waits for them, and re-layouts  47.2 us (16%)
  blocking collectives  41.2 us (14%)
  starting transfers between devices  14.6 us (5%)
  between operations  14.2 us (5%)
  matrix products  10.9 us (4%)
  other arithmetic  10.4 us (4%)
    all_gather x1, waiting for transfers between devices, per_device(): piece = lax.all_gather(received, 'tp', axis=2, tiled=True)  68.7 us
    unnamed x3, waiting for transfers between devices  58.1 us
    all_to_all x1, blocking collectives, per_device(): lax.all_to_all(sendbuf.reshape(EXPERTS, CAP, slice_width), 'ep', split_ax...  41.2 us
    unnamed x20, local copies, waits for them, and re-layouts  38.2 us
    all_to_all x1, waiting for transfers between devices, per_device(): lax.all_to_all(expert_out, 'ep', split_axis=1, concat_axis=0, tiled=True)  17.3 us
    all_to_all x1, starting transfers between devices, per_device(): lax.all_to_all(expert_out, 'ep', split_axis=1, concat_axis=0, tiled=True)  7.26 us
    all_to_all x1, starting transfers between devices, sent_to_all(): return lax.all_to_all(copies, axis, split_axis=0, concat_axis=0, tiled=True)  7.26 us
  transfers between devices with their start and end apart: 4, of which 3 were waited for; matrix products, arithmetic and copies ran while one was open for 5% of the time, Pallas kernels for 0%

commit v1 on v0

v1 whole, which is shorter than its diff:
```python
import functools

import jax
import jax.numpy as jnp
from jax import lax
from jax.experimental import pallas as pl
from jax.experimental.pallas import tpu as pltpu
from jax.sharding import PartitionSpec as P

MESH = pl.DeviceIdType.MESH
DRAFT = 8
SCALE = 2.827
BF16, F32 = jnp.bfloat16, jnp.float32


def signed_order(n):
    half = n // 2
    order = [half]
    for d in range(half - 1, 0, -1):
        order += [d, -d]
    return order + [0]


def kernel(cfg, tok_ref, wg_ref, wu_ref, wd_ref, logit_ref, ids_ref, len_ref, mask_ref, out_ref, count_ref,
           X, G, WG, WU, WD, ACC, P1, P2, RB1, RB2, F1, F2, C,
           tok_sem, wl_sem, wr_send, wr_recv, ag_send, ag_recv, h1_send, h1_recv, h2_send, h2_recv,
           f1_send, f1_recv, f2_send, f2_recv, c_send, c_recv, d_sem, dr_send, dr_recv):
    NX, NY, NC = cfg["nx"], cfg["ny"], cfg["chunks"]
    HX, HY = NX // 2, NY // 2
    rows = cfg["rows"]
    half = rows // 2
    kc = cfg["kc"]
    ncol = cfg["ncol"]
    hid = cfg["hid"]
    nexp = cfg["nexp"]
    n_ep = 2 * NX
    ep = lax.axis_index("ep")
    tp = lax.axis_index("tp")
    core = lax.rem(ep, 2)
    partner = {"ep": ep + 1 - 2 * core}

    def xdev(d):
        return {"ep": lax.rem(ep + (2 * d) % n_ep, n_ep)}

    def ydev(d):
        return {"tp": lax.rem(tp + d % NY, NY)}

    kk = signed_order(NY)

    pending = []

    def remote(src, dst, send, recv, dev):
        c = pltpu.make_async_remote_copy(src_ref=src, dst_ref=dst, send_sem=send, recv_sem=recv,
                                         device_id=dev, device_id_type=MESH)
        c.start()
        pending.append(c)
        return c

    tok = []
    for q in range(NC):
        c = pltpu.make_async_copy(tok_ref.at[:, pl.ds(q * kc, kc)], X.at[q, 0], tok_sem.at[q])
        c.start()
        tok.append(c)
    wl = []
    for q in range(NC):
        r = pl.ds(q * kc, kc)
        for i, (src, dst) in enumerate(((wg_ref, WG), (wu_ref, WU))):
            c = pltpu.make_async_copy(src.at[0, r], dst.at[0, r], wl_sem.at[q, i])
            c.start()
            wl.append(c)
    dl = []
    dcols = []
    for p in range(NY):
        col = pl.ds(pl.multiple_of(lax.rem(tp + kk[p] % NY, NY) * ncol, 128), ncol)
        dcols.append(col)
        c = pltpu.make_async_copy(wd_ref.at[0, :, col], WD.at[p, pl.ds(0, hid)], d_sem.at[p])
        c.start()
        dl.append(c)

    barrier = pltpu.get_barrier_semaphore()
    peers = [partner] + [xdev(d) for d in range(1, NX)] + [ydev(d) for d in range(1, NY)]
    for dev in peers:
        pl.semaphore_signal(barrier, inc=1, device_id=dev, device_id_type=MESH)

    logits = logit_ref[...]
    sig = 1.0 / (1.0 + jnp.exp(-logits))
    gates = SCALE * sig / jnp.sum(sig, axis=0, keepdims=True)
    lane = lax.broadcasted_iota(jnp.int32, (1, rows), 1)
    length = jnp.zeros((1, rows), jnp.int32)
    for r in range(rows // DRAFT):
        length = jnp.where(lane // DRAFT == r, len_ref[r], length)
    gates = jnp.where(lane % DRAFT < length, gates, 0.0)
    mrow = lax.broadcasted_iota(jnp.int32, mask_ref.shape, 0)
    mcol = lax.broadcasted_iota(jnp.int32, mask_ref.shape, 1)
    mlen = jnp.zeros(mask_ref.shape, jnp.int32)
    for r in range(rows // DRAFT):
        mlen = jnp.where(mrow == r, len_ref[r], mlen)
    passed = jnp.where(mcol < mlen, mask_ref[...], 0).astype(F32)
    run = passed[:, 0:1]
    local_count = run
    for j in range(1, DRAFT):
        run = run * passed[:, j:j + 1]
        local_count = local_count + run
    local_count = jnp.sum(local_count, axis=0, keepdims=True)
    feat = lax.broadcasted_iota(jnp.int32, (128, rows), 0)
    dense = jnp.zeros((128, rows), F32)
    ids = ids_ref[...]
    for k in range(ids.shape[0]):
        e = ids[k:k + 1, :]
        dense = dense + jnp.where((feat == e) | (feat == e + nexp), gates[k:k + 1, :], 0.0)
    high = dense.astype(BF16)
    packed = jnp.where(feat < nexp, high.astype(F32), dense - high.astype(F32))
    packed = packed + jnp.where(feat == 2 * nexp, local_count, 0.0)
    eye = (lax.broadcasted_iota(jnp.int32, (rows, rows), 0) == lax.broadcasted_iota(jnp.int32, (rows, rows), 1))
    turned = lax.dot_general(eye.astype(F32).astype(BF16), packed.astype(BF16), (((1,), (1,)), ((), ())),
                             preferred_element_type=F32)
    G[0] = turned.astype(BF16)

    pl.semaphore_wait(barrier, len(peers))

    wr = []
    for q in range(NC):
        r = pl.ds(q * kc, kc)
        for i, (src, dst) in enumerate(((wg_ref, WG), (wu_ref, WU))):
            wr.append(remote(src.at[0, r], dst.at[1, r], wr_send.at[q, i], wr_recv.at[q, i], partner))
    dr = []
    for p in range(NY):
        dr.append(remote(wd_ref.at[0, :, dcols[p]], WD.at[p, pl.ds(hid, hid)], dr_send.at[p], dr_recv.at[p], partner))

    ag = {}
    lo, hi = pl.ds(0, half), pl.ds(half, half)

    def view(q, slot, part):
        ref = G.at[slot] if q == NC else X.at[q, slot]
        return ref if part is None else ref.at[part]

    def ag_send_step(q, s):
        if s == 0:
            if q < NC:
                tok[q].wait()
        else:
            ag[q, s - 1, 0].wait_recv()
        ag[q, s, 0] = remote(view(q, s, lo if s == HX - 1 else None), view(q, s + 1, lo if s == HX - 1 else None),
                             ag_send.at[q, s, 0], ag_recv.at[q, s, 0], xdev(1))
        if s > 0:
            ag[q, s - 1, 1].wait_recv()
        a, b = (NX - s) % NX, NX - s - 1
        ag[q, s, 1] = remote(view(q, a, hi if s == HX - 1 else None), view(q, b, hi if s == HX - 1 else None),
                             ag_send.at[q, s, 1], ag_recv.at[q, s, 1], xdev(-1))

    def ag_finish(q):
        ag[q, HX - 1, 0].wait_recv()
        ag[q, HX - 1, 1].wait_recv()

    def gate_up(q):
        r = pl.ds(q * kc, kc)
        x = X[q].reshape(NX * rows, kc)
        for i, w in enumerate((WG, WU)):
            for e in range(2):
                (wl if e == 0 else wr)[2 * q + i].wait() if e == 0 else wr[2 * q + i].wait_recv()
                y = jnp.dot(x, w[e, r, :], preferred_element_type=F32)
                if q == 0:
                    ACC[i, e] = y
                else:
                    ACC[i, e] = ACC[i, e] + y

    first = NC // 2
    groups = [list(range(first)), list(range(first, NC)) + [NC]]
    for s in range(HX):
        for q in groups[0]:
            ag_send_step(q, s)
    for s in range(HX):
        for n, q in enumerate(groups[1]):
            ag_send_step(q, s)
        if s < len(groups[0]):
            ag_finish(groups[0][s])
            gate_up(groups[0][s])
    for q in groups[0][HX:]:
        ag_finish(q)
        gate_up(q)
    for q in groups[1]:
        ag_finish(q)
        if q < NC:
            gate_up(q)

    g_all = G[...].reshape(NX * rows, 128).astype(F32)
    glane = lax.broadcasted_iota(jnp.int32, (NX * rows, 128), 1)
    grow = lax.broadcasted_iota(jnp.int32, (NX * rows, 128), 0)
    tally = jnp.where((glane == 2 * nexp) & (grow % rows == 0), g_all, 0.0)
    C[0] = jnp.zeros((8, 128), F32) + jnp.sum(tally)
    c_copy = remote(C.at[0], C.at[1], c_send, c_recv, partner)
    hs = []
    for e in range(2):
        expert = ep if e == 0 else partner["ep"]
        gate = jnp.sum(jnp.where((glane == expert) | (glane == expert + nexp), g_all, 0.0), axis=1, keepdims=True)
        g, u = ACC[0, e], ACC[1, e]
        hs.append((gate * (g / (1.0 + jnp.exp(-g)) * u)).astype(BF16))
    h = jnp.concatenate(hs, axis=1)

    def down(p):
        dl[p].wait()
        dr[p].wait_recv()
        y = jnp.dot(h, WD[p], preferred_element_type=F32).astype(BF16).reshape(NX, rows, ncol)
        P1[p] = y[:, :half]
        P2[p] = y[:, half:]

    pos = {k: p for p, k in enumerate(kk)}
    NQ = NY // 2
    NJ = NX // 2
    h1, h2 = {}, {}

    def add(dst, src):
        dst[...] = (dst[...].astype(F32) + src[...].astype(F32)).astype(BF16)

    def h1_step(q, s):
        for d in range(2):
            slot = (HX + s) % NX if d == 0 else HX - s
            if s == 0:
                p, n = 2 * q + d, 1
            else:
                p, n = 2 * q, 2
                h1[q, s - 1, d].wait_recv()
                pa, na = (2 * q + d, 1) if s == 1 else (p, n)
                add(P1.at[pl.ds(pa, na), slot], RB1.at[d, s - 1, pl.ds(pa, na)])
            h1[q, s, d] = remote(P1.at[pl.ds(p, n), slot], RB1.at[d, s, pl.ds(p, n)],
                                 h1_send.at[q, s, d], h1_recv.at[q, s, d], xdev(1 if d == 0 else -1))

    def h2_step(j, s):
        for d in range(2):
            p = pos[HY - s] if (d == 0 or s == 0) else pos[s - HY]
            mine = (j < NJ // 2) == (d == 0)
            rng = pl.ds(2 * j, 2)
            if s == 0 and not mine:
                continue
            if s > 0 and (s > 1 or mine):
                h2[j, s - 1, d].wait_recv()
                add(P2.at[p, rng], RB2.at[d, s - 1, rng])
            h2[j, s, d] = remote(P2.at[p, rng], RB2.at[d, s, rng],
                                 h2_send.at[j, s, d], h2_recv.at[j, s, d], ydev(1 if d == 0 else -1))

    down(0)
    for j in range(NJ):
        h2_step(j, 0)
    down(1)
    h1_step(0, 0)
    for q in range(1, NQ):
        down(2 * q)
        down(2 * q + 1)
        h1_step(q, 0)
        if q == 1:
            for j in range(NJ):
                h2_step(j, 1)
    for s in range(1, HX):
        for i in range(max(NQ, NJ)):
            if i < NQ:
                h1_step(i, s)
            if i < NJ and s + 1 < HY:
                h2_step(i, s + 1)

    f1, f2 = [], []
    last = NY - 1

    def h1_final(q):
        h1[q, HX - 1, 0].wait_recv()
        h1[q, HX - 1, 1].wait_recv()
        r = pl.ds(2 * q, 2)
        P1[r, 0] = (P1[r, 0].astype(F32) + RB1[0, HX - 1, r].astype(F32) + RB1[1, HX - 1, r].astype(F32)).astype(BF16)
        for p in (2 * q, 2 * q + 1):
            if kk[p] != 0:
                f1.append(remote(P1.at[p, 0], F1.at[p], f1_send.at[p], f1_recv.at[p], ydev(kk[p])))

    def h2_final(j):
        h2[j, HY - 1, 0].wait_recv()
        h2[j, HY - 1, 1].wait_recv()
        r = pl.ds(2 * j, 2)
        P2[last, r] = (P2[last, r].astype(F32) + RB2[0, HY - 1, r].astype(F32) + RB2[1, HY - 1, r].astype(F32)).astype(BF16)
        for slot in (2 * j, 2 * j + 1):
            if slot != 0:
                f2.append(remote(P2.at[last, slot], F2.at[slot], f2_send.at[slot], f2_recv.at[slot], xdev(-slot)))

    for i in range(max(NQ, NJ)):
        if i < NJ:
            h2_final(i)
        if i < NQ:
            h1_final(i)

    for c in f1 + f2:
        c.wait_recv()
    a = P1[last, 0].astype(F32)
    for p in range(NY):
        if kk[p] != 0:
            a = a + F1[p].astype(F32)
    out_ref[pl.ds(0, half), :] = a.astype(BF16)
    b = P2[last, 0].astype(F32)
    for slot in range(1, NX):
        b = b + F2[slot].astype(F32)
    out_ref[pl.ds(half, half), :] = b.astype(BF16)
    c_copy.wait_recv()
    first_only = ((lax.broadcasted_iota(jnp.int32, (8, 128), 0) == 0)
                  & (lax.broadcasted_iota(jnp.int32, (8, 128), 1) == 0))
    count_ref[0] = jnp.sum(jnp.where(first_only, C[0] + C[1], 0.0)).astype(jnp.int32)
    for c in pending:
        c.wait_send()


def per_device(tokens, w_gate, w_up, w_down, router_logits, expert_ids, draft_lengths, accept_mask):
    nx, ny = lax.axis_size("ep") // 2, lax.axis_size("tp")
    rows, width = tokens.shape
    hid = w_gate.shape[2]
    ncol = width // ny
    chunks = ny
    kc = width // chunks
    half = rows // 2
    cfg = dict(nx=nx, ny=ny, chunks=chunks, rows=rows, kc=kc, ncol=ncol, hid=hid, nexp=lax.axis_size("ep"))
    hx, hy = nx // 2, ny // 2
    dma = pltpu.SemaphoreType.DMA
    scratch = [
        pltpu.VMEM((chunks, nx, rows, kc), BF16),
        pltpu.VMEM((nx, rows, 128), BF16),
        pltpu.VMEM((2, width, hid), BF16),
        pltpu.VMEM((2, width, hid), BF16),
        pltpu.VMEM((ny, 2 * hid, ncol), BF16),
        pltpu.VMEM((2, 2, nx * rows, hid), F32),
        pltpu.VMEM((ny, nx, half, ncol), BF16),
        pltpu.VMEM((ny, nx, half, ncol), BF16),
        pltpu.VMEM((2, hx, ny, half, ncol), BF16),
        pltpu.VMEM((2, hy, nx, half, ncol), BF16),
        pltpu.VMEM((ny, half, ncol), BF16),
        pltpu.VMEM((nx, half, ncol), BF16),
        pltpu.VMEM((2, 8, 128), F32),
        dma((chunks,)), dma((chunks, 2)), dma((chunks, 2)), dma((chunks, 2)),
        dma((chunks + 1, hx, 2)), dma((chunks + 1, hx, 2)),
        dma((ny // 2, hx, 2)), dma((ny // 2, hx, 2)), dma((nx // 2, hy, 2)), dma((nx // 2, hy, 2)),
        dma((ny,)), dma((ny,)), dma((nx,)), dma((nx,)), dma(()), dma(()), dma((ny,)), dma((ny,)), dma((ny,)),
    ]
    anyspec = pl.BlockSpec(memory_space=pl.ANY)
    vmem = pl.BlockSpec(memory_space=pltpu.VMEM)
    smem = pl.BlockSpec(memory_space=pltpu.SMEM)
    mixed, accepted = pl.pallas_call(
        functools.partial(kernel, cfg),
        out_shape=(jax.ShapeDtypeStruct((rows, ncol), BF16), jax.ShapeDtypeStruct((1,), jnp.int32)),
        in_specs=[anyspec] * 4 + [vmem, vmem, smem, vmem],
        out_specs=(vmem, smem),
        scratch_shapes=scratch,
        name="routed_experts",
        compiler_params=pltpu.CompilerParams(collective_id=0, has_side_effects=True, vmem_limit_bytes=60 * 1024 * 1024),
    )(tokens, w_gate, w_up, w_down, router_logits.T, expert_ids.T, draft_lengths, accept_mask)
    return mixed, accepted


def solution(mesh):
    placed = (
        P(("groups", "ep"), None),
        P("ep", None, "tp"),
        P("ep", None, "tp"),
        P("ep", "tp", None),
        P(("groups", "ep"), None),
        P(("groups", "ep"), None),
        P(("groups", "ep")),
        P(("groups", "ep"), None),
    )
    return jax.shard_map(
        per_device,
        mesh=mesh,
        in_specs=placed,
        out_specs=(P(("groups", "ep"), "tp"), P("groups")),
        check_vma=False,
    )
```

time: 288 us -> 99.3 us (0.34); the launches traced: 283 us -> 98.4 us
  waiting for transfers between devices: 144 us -> 0 us
  Pallas kernels: 0 us -> 94.5 us
  local copies, waits for them, and re-layouts: 47.2 us -> 1.45 us
  blocking collectives: 41.2 us -> 0 us
  starting transfers between devices: 14.6 us -> 0 us
  between operations: 14.2 us -> 2.39 us
  matrix products: 10.9 us -> 0 us
  other arithmetic: 10.4 us -> 0 us
    pallas_call x0 -> x1, Pallas kernels: none -> 94.5 us  [per_device(): pl.pallas_call(functools.partial(kernel, cfg), out_shape=(jax.ShapeDtypeS...]
    all_gather x1 -> x0, waiting for transfers between devices: 68.7 us -> none  [per_device(): piece = lax.all_gather(received, 'tp', axis=2, tiled=True)]
    unnamed x3 -> x0, waiting for transfers between devices: 58.1 us -> none
    all_to_all x1 -> x0, blocking collectives: 41.2 us -> none  [per_device(): lax.all_to_all(sendbuf.reshape(EXPERTS, CAP, slice_width), 'ep', split_ax...]
    unnamed x20 -> x1, local copies, waits for them, and re-layouts: 38.2 us -> 1.45 us
    all_to_all x2 -> x0, waiting for transfers between devices: 17.3 us -> none  [the longest x1 17.3 us: per_device(): lax.all_to_all(expert_out, 'ep', split_axis=1, concat_axis=0, tiled=True)]
    all_to_all x2 -> x0, starting transfers between devices: 14.5 us -> none  [the longest x1 7.26 us: per_device(): lax.all_to_all(expert_out, 'ep', split_axis=1, concat_axis=0, tiled=True)]
    dot_general x3 -> x0, matrix products: 10.9 us -> none  [the longest x1 5.39 us: per_device(): jnp.einsum('emd,edf->emf', piece, w_gate, preferred_element_type=jnp.floa...]
  transfers between devices with their start and end apart: 4 -> 0, of which waited for: 3 -> 0; matrix products, arithmetic and copies ran while one was open for 5% -> 0% of each run, Pallas kernels for 0% -> 0%
where the time goes in v1:
time: 99.3 us; the launch traced here: 98.4 us
  Pallas kernels  94.5 us (95%)
  between operations  2.39 us (2%)
  local copies, waits for them, and re-layouts  1.45 us (1%)
    pallas_call x1, Pallas kernels, per_device(): pl.pallas_call(functools.partial(kernel, cfg), out_shape=(jax.ShapeDtypeS...  94.5 us

profile of v1, /device:TPU:516, one launch (start us, length us, event | category | flops | bytes accessed | tf_op | source)
XLA Modules:
  0.0 98.4 jit_solution(9382232165216193224)
XLA Ops:
  0.6 94.5 %routed_experts.1 = (bf16[32,896]{1,0:T(8,128)(2,1)}, s32[1]{0:T(128)}) custom-call(bf16[32,7168]{1,0:T(8,128)(2,1)} %tok_ref.1, bf16[1,7168,256]{2,1,0:T(8,128)(2,1)} %wg_ref.1, bf16[1,7168,256]{2,1,0:T(8,128)(2,1)} %wu_ref.1, bf16[1,256,7168]{2,1,0:T(8,128)(2,1)} %wd_ref.1, f32[8,32]{1,0:T(8,128)} %bitcast.2, s32[8,32]{1,0:T(8,128)} %bitcast.3, s32[4]{0:T(128)} %len_ref.1, ...), custom_call_target="tpu_custom_call" | custom-call | tf_op jit(solution)/shard_map/routed_experts/pallas_call | solution.py:339
  95.2 1.4 %copy.12 = bf16[32,896]{1,0:T(8,128)(2,1)} copy(bf16[32,896]{1,0:T(8,128)(2,1)} %get-tuple-element.4) | data formatting | bytes 114688

commit v2 on v1

--- a/solution.py
+++ b/solution.py
@@ -21,19 +21,59 @@
     return order + [0]
 
 
+def gather_order(nx, ny, na, unit_a, unit_b, lat):
+    hx, hy = nx // 2, ny // 2
+    jobs = {}
+    for st in range(hx):
+        cut = 0.5 if st == hx - 1 else 1.0
+        for d in range(2):
+            for q in range(na):
+                jobs["a", q, st, d] = (d, unit_a * cut, ("a", q, st - 1, d) if st else None, 100 + q)
+            jobs["g", 0, st, d] = (d, unit_b * cut / 4, ("g", 0, st - 1, d) if st else None, 200)
+            if st < hx - 1 or d == 0:
+                jobs["b", 0, st, d] = (d, unit_b, ("b", 0, st - 1, d) if st else None, 0)
+    for j in range(1, nx):
+        dep = ("b", 0, j - 1, 0) if j <= hx else ("b", 0, nx - 1 - j, 1)
+        for d in range(2):
+            for st in range(hy):
+                if st < hy - 1 or j % 2 != d:
+                    jobs["y", j, st, d] = (2 + d, unit_b, dep if st == 0 else ("y", j, st - 1, d), -min(j, nx - j))
+    ready = {k: 0.0 for k, v in jobs.items() if v[2] is None}
+    free, order, arrive, left = [0.0] * 4, [], {}, set(jobs)
+    while left:
+        best = None
+        for link in range(4):
+            able = [k for k in left if jobs[k][0] == link and k in ready]
+            if able:
+                t = max(free[link], min(ready[k] for k in able))
+                k = min((k for k in able if ready[k] <= t + 1e-9), key=lambda k: (jobs[k][3], ready[k], k))
+                if best is None or t < best[0]:
+                    best = (t, k)
+        t, k = best
+        free[jobs[k][0]] = t + jobs[k][1]
+        arrive[k] = free[jobs[k][0]] + lat
+        order.append((t, k))
+        left.discard(k)
+        for m, v in jobs.items():
+            if v[2] == k:
+                ready[m] = arrive[k]
+    return sorted(order), {k: v[2] for k, v in jobs.items()}, arrive
+
+
 def kernel(cfg, tok_ref, wg_ref, wu_ref, wd_ref, logit_ref, ids_ref, len_ref, mask_ref, out_ref, count_ref,
-           X, G, WG, WU, WD, ACC, P1, P2, RB1, RB2, F1, F2, C,
-           tok_sem, wl_sem, wr_send, wr_recv, ag_send, ag_recv, h1_send, h1_recv, h2_send, h2_recv,
-           f1_send, f1_recv, f2_send, f2_recv, c_send, c_recv, d_sem, dr_send, dr_recv):
-    NX, NY, NC = cfg["nx"], cfg["ny"], cfg["chunks"]
+           XA, XB, G, W, WD, ACC, P1, P2, RB1, RB2, F1, F2, C,
+           ta_sem, tb_sem, wla_sem, wlb_sem, wra_sem, wrb_sem, a_recv, b_recv, g_recv, y_recv, h1_recv, h2_recv,
+           f1_recv, f2_recv, c_recv, d_sem, dr_recv, send_sem):
+    NX, NY, NA = cfg["nx"], cfg["ny"], cfg["na"]
     HX, HY = NX // 2, NY // 2
     rows = cfg["rows"]
     half = rows // 2
-    kc = cfg["kc"]
+    ka, kb = cfg["ka"], cfg["kb"]
     ncol = cfg["ncol"]
     hid = cfg["hid"]
     nexp = cfg["nexp"]
     n_ep = 2 * NX
+    base = NA * ka
     ep = lax.axis_index("ep")
     tp = lax.axis_index("tp")
     core = lax.rem(ep, 2)
@@ -45,40 +85,44 @@
     def ydev(d):
         return {"tp": lax.rem(tp + d % NY, NY)}
 
+    def slice_of(r, size, start=0):
+        return pl.ds(pl.multiple_of(start + lax.rem(tp + r % NY, NY) * size, 128), size)
+
     kk = signed_order(NY)
-
-    pending = []
+    A_SEND, B_SEND, G_SEND, Y_SEND, H1_SEND, H2_SEND, F1_SEND, F2_SEND, C_SEND, W_SEND, D_SEND = range(11)
 
     def remote(src, dst, send, recv, dev):
-        c = pltpu.make_async_remote_copy(src_ref=src, dst_ref=dst, send_sem=send, recv_sem=recv,
+        c = pltpu.make_async_remote_copy(src_ref=src, dst_ref=dst, send_sem=send_sem.at[send], recv_sem=recv,
                                          device_id=dev, device_id_type=MESH)
         c.start()
-        pending.append(c)
         return c
 
-    tok = []
-    for q in range(NC):
-        c = pltpu.make_async_copy(tok_ref.at[:, pl.ds(q * kc, kc)], X.at[q, 0], tok_sem.at[q])
+    tok_a, tok_b = [], []
+    for r in range(NY):
+        c = pltpu.make_async_copy(tok_ref.at[:, slice_of(r, kb, base)], XB.at[r, 0], tb_sem.at[r])
         c.start()
-        tok.append(c)
-    wl = []
-    for q in range(NC):
-        r = pl.ds(q * kc, kc)
-        for i, (src, dst) in enumerate(((wg_ref, WG), (wu_ref, WU))):
-            c = pltpu.make_async_copy(src.at[0, r], dst.at[0, r], wl_sem.at[q, i])
-            c.start()
-            wl.append(c)
+        tok_b.append(c)
+    for q in range(NA):
+        c = pltpu.make_async_copy(tok_ref.at[:, pl.ds(q * ka, ka)], XA.at[q, 0], ta_sem.at[q])
+        c.start()
+        tok_a.append(c)
+    rows_a = [pl.ds(q * ka, ka) for q in range(NA)]
+    rows_b = [pl.ds(base + r * kb, kb) for r in range(NY)]
+    from_b = [slice_of(r, kb, base) for r in range(NY)]
+    for src, dst, sem in ([(rows_a[q], rows_a[q], wla_sem.at[q]) for q in range(NA)]
+                          + [(from_b[r], rows_b[r], wlb_sem.at[r]) for r in range(NY)]):
+        for i, w in enumerate((wg_ref, wu_ref)):
+            pltpu.make_async_copy(w.at[0, src], W.at[0, i, dst], sem).start()
     dl = []
     dcols = []
     for p in range(NY):
-        col = pl.ds(pl.multiple_of(lax.rem(tp + kk[p] % NY, NY) * ncol, 128), ncol)
-        dcols.append(col)
-        c = pltpu.make_async_copy(wd_ref.at[0, :, col], WD.at[p, pl.ds(0, hid)], d_sem.at[p])
+        dcols.append(slice_of(kk[p], ncol))
+        c = pltpu.make_async_copy(wd_ref.at[0, :, dcols[p]], WD.at[p, pl.ds(0, hid)], d_sem.at[p])
         c.start()
         dl.append(c)
 
     barrier = pltpu.get_barrier_semaphore()
-    peers = [partner] + [xdev(d) for d in range(1, NX)] + [ydev(d) for d in range(1, NY)]
+    peers = [partner, xdev(1), xdev(-1), ydev(1), ydev(-1)]
     for dev in peers:
         pl.semaphore_signal(barrier, inc=1, device_id=dev, device_id_type=MESH)
 
@@ -118,77 +162,118 @@
 
     pl.semaphore_wait(barrier, len(peers))
 
-    wr = []
-    for q in range(NC):
-        r = pl.ds(q * kc, kc)
-        for i, (src, dst) in enumerate(((wg_ref, WG), (wu_ref, WU))):
-            wr.append(remote(src.at[0, r], dst.at[1, r], wr_send.at[q, i], wr_recv.at[q, i], partner))
+    lo, hi = pl.ds(0, half), pl.ds(half, half)
+    order, deps, arrive = gather_order(NX, NY, NA, cfg["ta"], cfg["tb"], cfg["lat"])
+    copies = {}
+    heard = set()
+
+    def hear(key):
+        if key not in heard:
+            heard.add(key)
+            copies[key].wait_recv()
+
+    def own_ready(kind, n):
+        if (kind, n) not in heard:
+            heard.add((kind, n))
+            (tok_a if kind == "a" else tok_b)[n].wait()
+
+    def send(key):
+        kind, n, st, d = key
+        if deps[key] is not None:
+            hear(deps[key])
+        last = st == HX - 1
+        if kind == "y":
+            r = (NY - st) % NY if d == 0 else st
+            to = NY - 1 - st if d == 0 else st + 1
+            copies[key] = remote(XB.at[r, n], XB.at[to, n], Y_SEND, y_recv.at[n, st, d], ydev(1 if d == 0 else -1))
+            return
+        a, b = (st, st + 1) if d == 0 else ((NX - st) % NX, NX - st - 1)
+        dev = xdev(1 if d == 0 else -1)
+        if kind == "b":
+            own_ready("b", 0)
+            copies[key] = remote(XB.at[0, a], XB.at[0, b], B_SEND, b_recv.at[st, d], dev)
+            return
+        ref, sem, recv = (XA.at[n], A_SEND, a_recv.at[n, st, d]) if kind == "a" else (G, G_SEND, g_recv.at[st, d])
+        if kind == "a":
+            own_ready("a", n)
+        src, dst = ref.at[a], ref.at[b]
+        if last:
+            part = lo if d == 0 else hi
+            src, dst = src.at[part], dst.at[part]
+        copies[key] = remote(src, dst, sem, recv, dev)
+
+    started = []
+
+    def gate_up(x, part, sem_l, sem_r):
+        for e in range(2):
+            both = W.at[e, :, part]
+            pltpu.make_async_copy(both, both, sem_l if e == 0 else sem_r).wait()
+            for i in range(2):
+                y = jnp.dot(x, W[e, i, part, :], preferred_element_type=F32)
+                ACC[i, e] = ACC[i, e] + y if started else y
+        started.append(1)
+
+    def gate_up_a(q):
+        for d in range(2):
+            for st in range(HX):
+                hear(("a", q, st, d))
+        gate_up(XA[q].reshape(NX * rows, ka), rows_a[q], wla_sem.at[q], wra_sem.at[q])
+
+    def keys_b(r):
+        keys = []
+        for j in range(1, NX):
+            for d in range(2):
+                st = NY - 1 - r if d == 0 else r - 1
+                if ("y", j, st, d) in deps:
+                    keys.append(("y", j, st, d))
+            if r == 0:
+                keys.append(("b", 0, j - 1, 0) if j <= HX else ("b", 0, NX - 1 - j, 1))
+        return keys
+
+    def gate_up_b(r):
+        own_ready("b", r)
+        for key in keys_b(r):
+            hear(key)
+        gate_up(XB[r].reshape(NX * rows, kb), rows_b[r], wlb_sem.at[r], wrb_sem.at[r])
+
+    work = []
+    for q in range(NA):
+        work.append((max(arrive["a", q, st, d] for st in range(HX) for d in range(2)), "ga", q))
+    for r in range(NY):
+        work.append((max(arrive[key] for key in keys_b(r)), "gb", r))
+    events = sorted([(t, 0, key) for t, key in order] + [(t, 1, (kind, n)) for t, kind, n in work])
+    sent = 0
     dr = []
-    for p in range(NY):
-        dr.append(remote(wd_ref.at[0, :, dcols[p]], WD.at[p, pl.ds(hid, hid)], dr_send.at[p], dr_recv.at[p], partner))
-
-    ag = {}
-    lo, hi = pl.ds(0, half), pl.ds(half, half)
-
-    def view(q, slot, part):
-        ref = G.at[slot] if q == NC else X.at[q, slot]
-        return ref if part is None else ref.at[part]
-
-    def ag_send_step(q, s):
-        if s == 0:
-            if q < NC:
-                tok[q].wait()
+    for t, which, key in events:
+        if which == 0:
+            send(key)
+            sent += 1
+        elif key[0] == "ga":
+            gate_up_a(key[1])
         else:
-            ag[q, s - 1, 0].wait_recv()
-        ag[q, s, 0] = remote(view(q, s, lo if s == HX - 1 else None), view(q, s + 1, lo if s == HX - 1 else None),
-                             ag_send.at[q, s, 0], ag_recv.at[q, s, 0], xdev(1))
-        if s > 0:
-            ag[q, s - 1, 1].wait_recv()
-        a, b = (NX - s) % NX, NX - s - 1
-        ag[q, s, 1] = remote(view(q, a, hi if s == HX - 1 else None), view(q, b, hi if s == HX - 1 else None),
-                             ag_send.at[q, s, 1], ag_recv.at[q, s, 1], xdev(-1))
-
-    def ag_finish(q):
-        ag[q, HX - 1, 0].wait_recv()
-        ag[q, HX - 1, 1].wait_recv()
-
-    def gate_up(q):
-        r = pl.ds(q * kc, kc)
-        x = X[q].reshape(NX * rows, kc)
-        for i, w in enumerate((WG, WU)):
-            for e in range(2):
-                (wl if e == 0 else wr)[2 * q + i].wait() if e == 0 else wr[2 * q + i].wait_recv()
-                y = jnp.dot(x, w[e, r, :], preferred_element_type=F32)
-                if q == 0:
-                    ACC[i, e] = y
+            gate_up_b(key[1])
+        if sent == 4 and not dr:
+            def push(src, dst, sem):
+                for i, w in enumerate((wg_ref, wu_ref)):
+                    remote(w.at[0, src], W.at[1, i, dst], W_SEND, sem, partner)
+
+            for _, kind, n in sorted(work):
+                if kind == "ga":
+                    push(rows_a[n], rows_a[n], wra_sem.at[n])
                 else:
-                    ACC[i, e] = ACC[i, e] + y
-
-    first = NC // 2
-    groups = [list(range(first)), list(range(first, NC)) + [NC]]
-    for s in range(HX):
-        for q in groups[0]:
-            ag_send_step(q, s)
-    for s in range(HX):
-        for n, q in enumerate(groups[1]):
-            ag_send_step(q, s)
-        if s < len(groups[0]):
-            ag_finish(groups[0][s])
-            gate_up(groups[0][s])
-    for q in groups[0][HX:]:
-        ag_finish(q)
-        gate_up(q)
-    for q in groups[1]:
-        ag_finish(q)
-        if q < NC:
-            gate_up(q)
+                    push(from_b[n], rows_b[n], wrb_sem.at[n])
+            for p in range(NY):
+                dr.append(remote(wd_ref.at[0, :, dcols[p]], WD.at[p, pl.ds(hid, hid)], D_SEND, dr_recv.at[p], partner))
+    for d in range(2):
+        for st in range(HX):
+            hear(("g", 0, st, d))
 
     g_all = G[...].reshape(NX * rows, 128).astype(F32)
     glane = lax.broadcasted_iota(jnp.int32, (NX * rows, 128), 1)
     grow = lax.broadcasted_iota(jnp.int32, (NX * rows, 128), 0)
     tally = jnp.where((glane == 2 * nexp) & (grow % rows == 0), g_all, 0.0)
     C[0] = jnp.zeros((8, 128), F32) + jnp.sum(tally)
-    c_copy = remote(C.at[0], C.at[1], c_send, c_recv, partner)
+    c_copy = remote(C.at[0], C.at[1], C_SEND, c_recv, partner)
     hs = []
     for e in range(2):
         expert = ep if e == 0 else partner["ep"]
@@ -223,7 +308,7 @@
                 pa, na = (2 * q + d, 1) if s == 1 else (p, n)
                 add(P1.at[pl.ds(pa, na), slot], RB1.at[d, s - 1, pl.ds(pa, na)])
             h1[q, s, d] = remote(P1.at[pl.ds(p, n), slot], RB1.at[d, s, pl.ds(p, n)],
-                                 h1_send.at[q, s, d], h1_recv.at[q, s, d], xdev(1 if d == 0 else -1))
+                                 H1_SEND, h1_recv.at[q, s, d], xdev(1 if d == 0 else -1))
 
     def h2_step(j, s):
         for d in range(2):
@@ -236,7 +321,7 @@
                 h2[j, s - 1, d].wait_recv()
                 add(P2.at[p, rng], RB2.at[d, s - 1, rng])
             h2[j, s, d] = remote(P2.at[p, rng], RB2.at[d, s, rng],
-                                 h2_send.at[j, s, d], h2_recv.at[j, s, d], ydev(1 if d == 0 else -1))
+                                 H2_SEND, h2_recv.at[j, s, d], ydev(1 if d == 0 else -1))
 
     down(0)
     for j in range(NJ):
@@ -267,7 +352,7 @@
         P1[r, 0] = (P1[r, 0].astype(F32) + RB1[0, HX - 1, r].astype(F32) + RB1[1, HX - 1, r].astype(F32)).astype(BF16)
         for p in (2 * q, 2 * q + 1):
             if kk[p] != 0:
-                f1.append(remote(P1.at[p, 0], F1.at[p], f1_send.at[p], f1_recv.at[p], ydev(kk[p])))
+                f1.append(remote(P1.at[p, 0], F1.at[p], F1_SEND, f1_recv.at[p], ydev(kk[p])))
 
     def h2_final(j):
         h2[j, HY - 1, 0].wait_recv()
@@ -276,7 +361,7 @@
         P2[last, r] = (P2[last, r].astype(F32) + RB2[0, HY - 1, r].astype(F32) + RB2[1, HY - 1, r].astype(F32)).astype(BF16)
         for slot in (2 * j, 2 * j + 1):
             if slot != 0:
-                f2.append(remote(P2.at[last, slot], F2.at[slot], f2_send.at[slot], f2_recv.at[slot], xdev(-slot)))
+                f2.append(remote(P2.at[last, slot], F2.at[slot], F2_SEND, f2_recv.at[slot], xdev(-slot)))
 
     for i in range(max(NQ, NJ)):
         if i < NJ:
@@ -299,8 +384,22 @@
     first_only = ((lax.broadcasted_iota(jnp.int32, (8, 128), 0) == 0)
                   & (lax.broadcasted_iota(jnp.int32, (8, 128), 1) == 0))
     count_ref[0] = jnp.sum(jnp.where(first_only, C[0] + C[1], 0.0)).astype(jnp.int32)
-    for c in pending:
-        c.wait_send()
+
+    def drained(sem, ref):
+        pltpu.make_async_copy(ref, ref, send_sem.at[sem]).wait()
+
+    most = pl.ds(0, NX - 1)
+    drained(A_SEND, XA.at[:, most])
+    drained(B_SEND, XB.at[0, most])
+    drained(G_SEND, G.at[most])
+    drained(Y_SEND, XB.at[pl.ds(0, NY - 1), most])
+    drained(W_SEND, W.at[1])
+    drained(D_SEND, WD.at[:, pl.ds(0, hid)])
+    drained(C_SEND, C.at[0])
+    drained(H1_SEND, P1.at[:, most])
+    drained(H2_SEND, P2.at[pl.ds(0, NY - 1)])
+    drained(F1_SEND, F1.at[pl.ds(0, NY - 1)])
+    drained(F2_SEND, F2.at[most])
 
 
 def per_device(tokens, w_gate, w_up, w_down, router_logits, expert_ids, draft_lengths, accept_mask):
@@ -308,17 +407,20 @@
     rows, width = tokens.shape
     hid = w_gate.shape[2]
     ncol = width // ny
-    chunks = ny
-    kc = width // chunks
     half = rows // 2
-    cfg = dict(nx=nx, ny=ny, chunks=chunks, rows=rows, kc=kc, ncol=ncol, hid=hid, nexp=lax.axis_size("ep"))
     hx, hy = nx // 2, ny // 2
+    kb = 512
+    na = 3
+    ka = (width - ny * kb) // na
+    us_per_col = rows * 2 / 46.6e3
+    cfg = dict(nx=nx, ny=ny, na=na, ka=ka, kb=kb, rows=rows, ncol=ncol, hid=hid, nexp=lax.axis_size("ep"),
+               ta=ka * us_per_col, tb=kb * us_per_col, lat=2.0)
     dma = pltpu.SemaphoreType.DMA
     scratch = [
-        pltpu.VMEM((chunks, nx, rows, kc), BF16),
+        pltpu.VMEM((na, nx, rows, ka), BF16),
+        pltpu.VMEM((ny, nx, rows, kb), BF16),
         pltpu.VMEM((nx, rows, 128), BF16),
-        pltpu.VMEM((2, width, hid), BF16),
-        pltpu.VMEM((2, width, hid), BF16),
+        pltpu.VMEM((2, 2, width, hid), BF16),
         pltpu.VMEM((ny, 2 * hid, ncol), BF16),
         pltpu.VMEM((2, 2, nx * rows, hid), F32),
         pltpu.VMEM((ny, nx, half, ncol), BF16),
@@ -328,10 +430,9 @@
         pltpu.VMEM((ny, half, ncol), BF16),
         pltpu.VMEM((nx, half, ncol), BF16),
         pltpu.VMEM((2, 8, 128), F32),
-        dma((chunks,)), dma((chunks, 2)), dma((chunks, 2)), dma((chunks, 2)),
-        dma((chunks + 1, hx, 2)), dma((chunks + 1, hx, 2)),
-        dma((ny // 2, hx, 2)), dma((ny // 2, hx, 2)), dma((nx // 2, hy, 2)), dma((nx // 2, hy, 2)),
-        dma((ny,)), dma((ny,)), dma((nx,)), dma((nx,)), dma(()), dma(()), dma((ny,)), dma((ny,)), dma((ny,)),
+        dma((na,)), dma((ny,)), dma((na,)), dma((ny,)), dma((na,)), dma((ny,)),
+        dma((na, hx, 2)), dma((hx, 2)), dma((hx, 2)), dma((nx, hy, 2)), dma((ny // 2, hx, 2)), dma((nx // 2, hy, 2)),
+        dma((ny,)), dma((nx,)), dma(()), dma((ny,)), dma((ny,)), dma((11,)),
     ]
     anyspec = pl.BlockSpec(memory_space=pl.ANY)
     vmem = pl.BlockSpec(memory_space=pltpu.VMEM)

time: 99.3 us -> 89.3 us (0.90)
  Pallas kernels: 94.5 us -> 84.2 us
    pallas_call x1, Pallas kernels: 94.5 us -> 84.2 us  [per_device(): pl.pallas_call(functools.partial(kernel, cfg), out_shape=(jax.ShapeDtypeS...]
where the time goes in v2:
time: 89.3 us; the launch traced here: 88 us
  Pallas kernels  84.2 us (94%)
  between operations  2.39 us (3%)
  local copies, waits for them, and re-layouts  1.45 us (2%)
    pallas_call x1, Pallas kernels, per_device(): pl.pallas_call(functools.partial(kernel, cfg), out_shape=(jax.ShapeDtypeS...  84.2 us

profile of v2, /device:TPU:516, one launch (start us, length us, event | category | flops | bytes accessed | tf_op | source)
XLA Modules:
  0.0 88.0 jit_solution(16460126875419797057)
XLA Ops:
  0.6 84.2 %routed_experts.1 = (bf16[32,896]{1,0:T(8,128)(2,1)}, s32[1]{0:T(128)}) custom-call(bf16[32,7168]{1,0:T(8,128)(2,1)} %tok_ref.1, bf16[1,7168,256]{2,1,0:T(8,128)(2,1)} %wg_ref.1, bf16[1,7168,256]{2,1,0:T(8,128)(2,1)} %wu_ref.1, bf16[1,256,7168]{2,1,0:T(8,128)(2,1)} %wd_ref.1, f32[8,32]{1,0:T(8,128)} %bitcast.2, s32[8,32]{1,0:T(8,128)} %bitcast.3, s32[4]{0:T(128)} %len_ref.1, ...), custom_call_target="tpu_custom_call" | custom-call | tf_op jit(solution)/shard_map/routed_experts/pallas_call | solution.py:440
  84.8 1.4 %copy.12 = bf16[32,896]{1,0:T(8,128)(2,1)} copy(bf16[32,896]{1,0:T(8,128)(2,1)} %get-tuple-element.4) | data formatting | bytes 114688

commit v3 on v2

--- a/solution.py
+++ b/solution.py
@@ -241,29 +241,36 @@
         work.append((max(arrive["a", q, st, d] for st in range(HX) for d in range(2)), "ga", q))
     for r in range(NY):
         work.append((max(arrive[key] for key in keys_b(r)), "gb", r))
-    events = sorted([(t, 0, key) for t, key in order] + [(t, 1, (kind, n)) for t, kind, n in work])
-    sent = 0
+    pushes, clock = [], 0.0
+    for need, kind, n in sorted(work):
+        for i in range(2):
+            pushes.append((min(clock, need - 3.0), "w", (kind, n, i)))
+            clock += (ka if kind == "ga" else kb) * hid * 2 / cfg["push_rate"]
+    for p in range(NY):
+        pushes.append((clock, "d", p))
+        clock += ncol * hid * 2 / cfg["push_rate"]
     dr = []
-    for t, which, key in events:
-        if which == 0:
-            send(key)
-            sent += 1
-        elif key[0] == "ga":
-            gate_up_a(key[1])
+
+    def push(kind, what):
+        if kind == "d":
+            dr.append(remote(wd_ref.at[0, :, dcols[what]], WD.at[what, pl.ds(hid, hid)], D_SEND, dr_recv.at[what], partner))
+            return
+        group, n, i = what
+        src, dst, sem = (rows_a[n], rows_a[n], wra_sem.at[n]) if group == "ga" else (from_b[n], rows_b[n], wrb_sem.at[n])
+        remote((wg_ref, wu_ref)[i].at[0, src], W.at[1, i, dst], W_SEND, sem, partner)
+
+    events = sorted([(t, 1, n, ("s", key)) for n, (t, key) in enumerate(order)]
+                    + [(t, 2, n, (kind, what)) for n, (t, kind, what) in enumerate(work)]
+                    + [(t, 0, n, (kind, what)) for n, (t, kind, what) in enumerate(pushes)])
+    for _, _, _, (kind, what) in events:
+        if kind == "s":
+            send(what)
+        elif kind == "ga":
+            gate_up_a(what)
+        elif kind == "gb":
+            gate_up_b(what)
         else:
-            gate_up_b(key[1])
-        if sent == 4 and not dr:
-            def push(src, dst, sem):
-                for i, w in enumerate((wg_ref, wu_ref)):
-                    remote(w.at[0, src], W.at[1, i, dst], W_SEND, sem, partner)
-
-            for _, kind, n in sorted(work):
-                if kind == "ga":
-                    push(rows_a[n], rows_a[n], wra_sem.at[n])
-                else:
-                    push(from_b[n], rows_b[n], wrb_sem.at[n])
-            for p in range(NY):
-                dr.append(remote(wd_ref.at[0, :, dcols[p]], WD.at[p, pl.ds(hid, hid)], D_SEND, dr_recv.at[p], partner))
+            push(kind, what)
     for d in range(2):
         for st in range(HX):
             hear(("g", 0, st, d))
@@ -414,7 +421,8 @@
     ka = (width - ny * kb) // na
     us_per_col = rows * 2 / 46.6e3
     cfg = dict(nx=nx, ny=ny, na=na, ka=ka, kb=kb, rows=rows, ncol=ncol, hid=hid, nexp=lax.axis_size("ep"),
-               ta=ka * us_per_col, tb=kb * us_per_col, lat=2.0)
+               ta=ka * us_per_col, tb=kb * us_per_col, lat=2.0,
+               push_rate=450e3)
     dma = pltpu.SemaphoreType.DMA
     scratch = [
         pltpu.VMEM((na, nx, rows, ka), BF16),

time: 89.3 us -> 89.3 us (level)
  no operation moved by 1% of the time
where the time goes in v3:
time: 89.3 us; the launch traced here: 88 us
  Pallas kernels  84.2 us (94%)
  between operations  2.39 us (3%)
  local copies, waits for them, and re-layouts  1.45 us (2%)
    pallas_call x1, Pallas kernels, per_device(): pl.pallas_call(functools.partial(kernel, cfg), out_shape=(jax.ShapeDtypeS...  84.2 us

profile of v3, /device:TPU:516, one launch (start us, length us, event | category | flops | bytes accessed | tf_op | source)
XLA Modules:
  0.0 88.0 jit_solution(17420878633130141562)
XLA Ops:
  0.6 84.2 %routed_experts.1 = (bf16[32,896]{1,0:T(8,128)(2,1)}, s32[1]{0:T(128)}) custom-call(bf16[32,7168]{1,0:T(8,128)(2,1)} %tok_ref.1, bf16[1,7168,256]{2,1,0:T(8,128)(2,1)} %wg_ref.1, bf16[1,7168,256]{2,1,0:T(8,128)(2,1)} %wu_ref.1, bf16[1,256,7168]{2,1,0:T(8,128)(2,1)} %wd_ref.1, f32[8,32]{1,0:T(8,128)} %bitcast.2, s32[8,32]{1,0:T(8,128)} %bitcast.3, s32[4]{0:T(128)} %len_ref.1, ...), custom_call_target="tpu_custom_call" | custom-call | tf_op jit(solution)/shard_map/routed_experts/pallas_call | solution.py:448
  84.8 1.4 %copy.12 = bf16[32,896]{1,0:T(8,128)(2,1)} copy(bf16[32,896]{1,0:T(8,128)(2,1)} %get-tuple-element.4) | data formatting | bytes 114688

commit v4 on v3

--- a/solution.py
+++ b/solution.py
@@ -21,50 +21,74 @@
     return order + [0]
 
 
-def gather_order(nx, ny, na, unit_a, unit_b, lat):
-    hx, hy = nx // 2, ny // 2
+def gather_jobs(nx, na, ka, nb, nsub, kb, us_per_col, us_dot):
+    hx = nx // 2
     jobs = {}
     for st in range(hx):
         cut = 0.5 if st == hx - 1 else 1.0
         for d in range(2):
             for q in range(na):
-                jobs["a", q, st, d] = (d, unit_a * cut, ("a", q, st - 1, d) if st else None, 100 + q)
-            jobs["g", 0, st, d] = (d, unit_b * cut / 4, ("g", 0, st - 1, d) if st else None, 200)
-            if st < hx - 1 or d == 0:
-                jobs["b", 0, st, d] = (d, unit_b, ("b", 0, st - 1, d) if st else None, 0)
+                jobs["a", q, st, d] = (d, ka * us_per_col * cut, [("a", q, st - 1, d)] if st else [], 100 + q)
+            for n in range(nsub):
+                jobs["b", n, st, d] = (d, kb / nsub * us_per_col * cut, [("b", n, st - 1, d)] if st else [], 0.1 * n)
+            jobs["g", 0, st, d] = (d, 128 * us_per_col * cut, [("g", 0, st - 1, d)] if st else [], 1)
     for j in range(1, nx):
-        dep = ("b", 0, j - 1, 0) if j <= hx else ("b", 0, nx - 1 - j, 1)
-        for d in range(2):
-            for st in range(hy):
-                if st < hy - 1 or j % 2 != d:
-                    jobs["y", j, st, d] = (2 + d, unit_b, dep if st == 0 else ("y", j, st - 1, d), -min(j, nx - j))
-    ready = {k: 0.0 for k, v in jobs.items() if v[2] is None}
-    free, order, arrive, left = [0.0] * 4, [], {}, set(jobs)
-    while left:
+        for n in range(nsub):
+            dep = [("b", n, st, d) for st, d in ((j - 1, 0), (nx - 1 - j, 1)) if st < hx]
+            for d in range(2):
+                far = min(j, nx - j)
+                jobs["y", n, j, 0, d] = (2 + d, kb / nsub * us_per_col, dep, 10 - far)
+                jobs["y", n, j, 1, d] = (2 + d, kb / nsub * us_per_col / 2, [("y", n, j, 0, d)], 9 - far)
+    for q in range(na):
+        jobs["ga", q] = (4, us_dot * ka, [("a", q, st, d) for st in range(hx) for d in range(2)], 500)
+    slots, subs = range(1, nx), range(nsub)
+    for r in range(nb):
+        if r == 0:
+            deps = [("b", n, st, d) for n in subs for st in range(hx) for d in range(2)]
+        elif r == 2:
+            deps = [("y", n, j, 1, d) for n in subs for j in slots for d in range(2)]
+        else:
+            deps = [("y", n, j, 0, 0 if r == 3 else 1) for n in subs for j in slots]
+        jobs["gb", r] = (4, us_dot * kb, deps, 500)
+    return jobs
+
+
+def plan(jobs, lat):
+    missing = {k: len(v[2]) for k, v in jobs.items()}
+    users = {}
+    for k, v in jobs.items():
+        for dep in v[2]:
+            users.setdefault(dep, []).append(k)
+    resources = range(5)
+    able = {r: [k for k in jobs if jobs[k][0] == r and not missing[k]] for r in resources}
+    when = {k: 0.0 for k in jobs}
+    free, order = [0.0 for _ in resources], []
+    while len(order) < len(jobs):
         best = None
-        for link in range(4):
-            able = [k for k in left if jobs[k][0] == link and k in ready]
-            if able:
-                t = max(free[link], min(ready[k] for k in able))
-                k = min((k for k in able if ready[k] <= t + 1e-9), key=lambda k: (jobs[k][3], ready[k], k))
+        for r in resources:
+            if able[r]:
+                t = max(free[r], min(when[k] for k in able[r]))
+                k = min((k for k in able[r] if when[k] <= t + 1e-9), key=lambda k: (jobs[k][3], when[k], k))
                 if best is None or t < best[0]:
                     best = (t, k)
         t, k = best
-        free[jobs[k][0]] = t + jobs[k][1]
-        arrive[k] = free[jobs[k][0]] + lat
+        r = jobs[k][0]
+        able[r].remove(k)
+        free[r] = t + jobs[k][1]
         order.append((t, k))
-        left.discard(k)
-        for m, v in jobs.items():
-            if v[2] == k:
-                ready[m] = arrive[k]
-    return sorted(order), {k: v[2] for k, v in jobs.items()}, arrive
+        for m in users.get(k, []):
+            when[m] = max(when[m], free[r] + (0.0 if r == 4 else lat))
+            missing[m] -= 1
+            if not missing[m]:
+                able[jobs[m][0]].append(m)
+    return order
 
 
 def kernel(cfg, tok_ref, wg_ref, wu_ref, wd_ref, logit_ref, ids_ref, len_ref, mask_ref, out_ref, count_ref,
            XA, XB, G, W, WD, ACC, P1, P2, RB1, RB2, F1, F2, C,
            ta_sem, tb_sem, wla_sem, wlb_sem, wra_sem, wrb_sem, a_recv, b_recv, g_recv, y_recv, h1_recv, h2_recv,
            f1_recv, f2_recv, c_recv, d_sem, dr_recv, send_sem):
-    NX, NY, NA = cfg["nx"], cfg["ny"], cfg["na"]
+    NX, NY, NA, NB, NSUB = cfg["nx"], cfg["ny"], cfg["na"], cfg["nb"], cfg["nsub"]
     HX, HY = NX // 2, NY // 2
     rows = cfg["rows"]
     half = rows // 2
@@ -85,8 +109,8 @@
     def ydev(d):
         return {"tp": lax.rem(tp + d % NY, NY)}
 
-    def slice_of(r, size, start=0):
-        return pl.ds(pl.multiple_of(start + lax.rem(tp + r % NY, NY) * size, 128), size)
+    def slice_of(r, count, size, start=0):
+        return pl.ds(pl.multiple_of(start + lax.rem(tp + r % count, count) * size, 128), size)
 
     kk = signed_order(NY)
     A_SEND, B_SEND, G_SEND, Y_SEND, H1_SEND, H2_SEND, F1_SEND, F2_SEND, C_SEND, W_SEND, D_SEND = range(11)
@@ -98,8 +122,8 @@
         return c
 
     tok_a, tok_b = [], []
-    for r in range(NY):
-        c = pltpu.make_async_copy(tok_ref.at[:, slice_of(r, kb, base)], XB.at[r, 0], tb_sem.at[r])
+    for r in range(NB):
+        c = pltpu.make_async_copy(tok_ref.at[:, slice_of(r, NB, kb, base)], XB.at[r, 0], tb_sem.at[r])
         c.start()
         tok_b.append(c)
     for q in range(NA):
@@ -107,16 +131,16 @@
         c.start()
         tok_a.append(c)
     rows_a = [pl.ds(q * ka, ka) for q in range(NA)]
-    rows_b = [pl.ds(base + r * kb, kb) for r in range(NY)]
-    from_b = [slice_of(r, kb, base) for r in range(NY)]
+    rows_b = [pl.ds(base + r * kb, kb) for r in range(NB)]
+    from_b = [slice_of(r, NB, kb, base) for r in range(NB)]
     for src, dst, sem in ([(rows_a[q], rows_a[q], wla_sem.at[q]) for q in range(NA)]
-                          + [(from_b[r], rows_b[r], wlb_sem.at[r]) for r in range(NY)]):
+                          + [(from_b[r], rows_b[r], wlb_sem.at[r]) for r in range(NB)]):
         for i, w in enumerate((wg_ref, wu_ref)):
             pltpu.make_async_copy(w.at[0, src], W.at[0, i, dst], sem).start()
     dl = []
     dcols = []
     for p in range(NY):
-        dcols.append(slice_of(kk[p], ncol))
+        dcols.append(slice_of(kk[p], NY, ncol))
         c = pltpu.make_async_copy(wd_ref.at[0, :, dcols[p]], WD.at[p, pl.ds(0, hid)], d_sem.at[p])
         c.start()
         dl.append(c)
@@ -163,7 +187,8 @@
     pl.semaphore_wait(barrier, len(peers))
 
     lo, hi = pl.ds(0, half), pl.ds(half, half)
-    order, deps, arrive = gather_order(NX, NY, NA, cfg["ta"], cfg["tb"], cfg["lat"])
+    jobs = gather_jobs(NX, NA, ka, NB, NSUB, kb, cfg["us_per_col"], cfg["us_dot"])
+    order = plan(jobs, cfg["lat"])
     copies = {}
     heard = set()
 
@@ -178,29 +203,29 @@
             (tok_a if kind == "a" else tok_b)[n].wait()
 
     def send(key):
-        kind, n, st, d = key
-        if deps[key] is not None:
-            hear(deps[key])
-        last = st == HX - 1
+        kind, n, st, d = key[0], key[1], key[-2], key[-1]
+        for dep in jobs[key][2]:
+            hear(dep)
+        part = lo if d == 0 else hi
+        cols = pl.ds(n * (kb // NSUB), kb // NSUB)
         if kind == "y":
-            r = (NY - st) % NY if d == 0 else st
-            to = NY - 1 - st if d == 0 else st + 1
-            copies[key] = remote(XB.at[r, n], XB.at[to, n], Y_SEND, y_recv.at[n, st, d], ydev(1 if d == 0 else -1))
+            j = key[2]
+            r, to = ((0, 3), (3, 2))[st] if d == 0 else ((0, 1), (1, 2))[st]
+            take = part if st == 1 else pl.ds(0, rows)
+            copies[key] = remote(XB.at[r, j, take, cols], XB.at[to, j, take, cols], Y_SEND, y_recv.at[n, j, st, d],
+                                 ydev(1 if d == 0 else -1))
             return
         a, b = (st, st + 1) if d == 0 else ((NX - st) % NX, NX - st - 1)
-        dev = xdev(1 if d == 0 else -1)
-        if kind == "b":
-            own_ready("b", 0)
-            copies[key] = remote(XB.at[0, a], XB.at[0, b], B_SEND, b_recv.at[st, d], dev)
-            return
-        ref, sem, recv = (XA.at[n], A_SEND, a_recv.at[n, st, d]) if kind == "a" else (G, G_SEND, g_recv.at[st, d])
+        take = part if st == HX - 1 else pl.ds(0, rows)
         if kind == "a":
             own_ready("a", n)
-        src, dst = ref.at[a], ref.at[b]
-        if last:
-            part = lo if d == 0 else hi
-            src, dst = src.at[part], dst.at[part]
-        copies[key] = remote(src, dst, sem, recv, dev)
+            src, dst, sem, recv = XA.at[n, a, take], XA.at[n, b, take], A_SEND, a_recv.at[n, st, d]
+        elif kind == "b":
+            own_ready("b", 0)
+            src, dst, sem, recv = XB.at[0, a, take, cols], XB.at[0, b, take, cols], B_SEND, b_recv.at[n, st, d]
+        else:
+            src, dst, sem, recv = G.at[a, take], G.at[b, take], G_SEND, g_recv.at[st, d]
+        copies[key] = remote(src, dst, sem, recv, xdev(1 if d == 0 else -1))
 
     started = []
 
@@ -213,36 +238,18 @@
                 ACC[i, e] = ACC[i, e] + y if started else y
         started.append(1)
 
-    def gate_up_a(q):
-        for d in range(2):
-            for st in range(HX):
-                hear(("a", q, st, d))
-        gate_up(XA[q].reshape(NX * rows, ka), rows_a[q], wla_sem.at[q], wra_sem.at[q])
-
-    def keys_b(r):
-        keys = []
-        for j in range(1, NX):
-            for d in range(2):
-                st = NY - 1 - r if d == 0 else r - 1
-                if ("y", j, st, d) in deps:
-                    keys.append(("y", j, st, d))
-            if r == 0:
-                keys.append(("b", 0, j - 1, 0) if j <= HX else ("b", 0, NX - 1 - j, 1))
-        return keys
-
-    def gate_up_b(r):
-        own_ready("b", r)
-        for key in keys_b(r):
-            hear(key)
-        gate_up(XB[r].reshape(NX * rows, kb), rows_b[r], wlb_sem.at[r], wrb_sem.at[r])
-
-    work = []
-    for q in range(NA):
-        work.append((max(arrive["a", q, st, d] for st in range(HX) for d in range(2)), "ga", q))
-    for r in range(NY):
-        work.append((max(arrive[key] for key in keys_b(r)), "gb", r))
+    def gate_up_step(key):
+        kind, n = key
+        for dep in jobs[key][2]:
+            hear(dep)
+        own_ready(kind[1], n)
+        if kind == "ga":
+            gate_up(XA[n].reshape(NX * rows, ka), rows_a[n], wla_sem.at[n], wra_sem.at[n])
+        else:
+            gate_up(XB[n].reshape(NX * rows, kb), rows_b[n], wlb_sem.at[n], wrb_sem.at[n])
+
     pushes, clock = [], 0.0
-    for need, kind, n in sorted(work):
+    for need, (kind, n) in [(t, key) for t, key in order if jobs[key][0] == 4]:
         for i in range(2):
             pushes.append((min(clock, need - 3.0), "w", (kind, n, i)))
             clock += (ka if kind == "ga" else kb) * hid * 2 / cfg["push_rate"]
@@ -260,17 +267,14 @@
         remote((wg_ref, wu_ref)[i].at[0, src], W.at[1, i, dst], W_SEND, sem, partner)
 
     events = sorted([(t, 1, n, ("s", key)) for n, (t, key) in enumerate(order)]
-                    + [(t, 2, n, (kind, what)) for n, (t, kind, what) in enumerate(work)]
                     + [(t, 0, n, (kind, what)) for n, (t, kind, what) in enumerate(pushes)])
     for _, _, _, (kind, what) in events:
-        if kind == "s":
+        if kind != "s":
+            push(kind, what)
+        elif jobs[what][0] == 4:
+            gate_up_step(what)
+        else:
             send(what)
-        elif kind == "ga":
-            gate_up_a(what)
-        elif kind == "gb":
-            gate_up_b(what)
-        else:
-            push(kind, what)
     for d in range(2):
         for st in range(HX):
             hear(("g", 0, st, d))
@@ -399,7 +403,7 @@
     drained(A_SEND, XA.at[:, most])
     drained(B_SEND, XB.at[0, most])
     drained(G_SEND, G.at[most])
-    drained(Y_SEND, XB.at[pl.ds(0, NY - 1), most])
+    drained(Y_SEND, XB.at[pl.ds(0, 3), most])
     drained(W_SEND, W.at[1])
     drained(D_SEND, WD.at[:, pl.ds(0, hid)])
     drained(C_SEND, C.at[0])
@@ -416,17 +420,16 @@
     ncol = width // ny
     half = rows // 2
     hx, hy = nx // 2, ny // 2
-    kb = 512
+    nb, nsub, kb = 4, 2, 1024
     na = 3
-    ka = (width - ny * kb) // na
+    ka = (width - nb * kb) // na
     us_per_col = rows * 2 / 46.6e3
-    cfg = dict(nx=nx, ny=ny, na=na, ka=ka, kb=kb, rows=rows, ncol=ncol, hid=hid, nexp=lax.axis_size("ep"),
-               ta=ka * us_per_col, tb=kb * us_per_col, lat=2.0,
-               push_rate=450e3)
+    cfg = dict(nx=nx, ny=ny, na=na, ka=ka, nb=nb, nsub=nsub, kb=kb, rows=rows, ncol=ncol, hid=hid,
+               nexp=lax.axis_size("ep"), us_per_col=us_per_col, us_dot=0.6e-3, lat=3.2, push_rate=450e3)
     dma = pltpu.SemaphoreType.DMA
     scratch = [
         pltpu.VMEM((na, nx, rows, ka), BF16),
-        pltpu.VMEM((ny, nx, rows, kb), BF16),
+        pltpu.VMEM((nb, nx, rows, kb), BF16),
         pltpu.VMEM((nx, rows, 128), BF16),
         pltpu.VMEM((2, 2, width, hid), BF16),
         pltpu.VMEM((ny, 2 * hid, ncol), BF16),
@@ -438,8 +441,8 @@
         pltpu.VMEM((ny, half, ncol), BF16),
         pltpu.VMEM((nx, half, ncol), BF16),
         pltpu.VMEM((2, 8, 128), F32),
-        dma((na,)), dma((ny,)), dma((na,)), dma((ny,)), dma((na,)), dma((ny,)),
-        dma((na, hx, 2)), dma((hx, 2)), dma((hx, 2)), dma((nx, hy, 2)), dma((ny // 2, hx, 2)), dma((nx // 2, hy, 2)),
+        dma((na,)), dma((nb,)), dma((na,)), dma((nb,)), dma((na,)), dma((nb,)),
+        dma((na, hx, 2)), dma((nsub, hx, 2)), dma((hx, 2)), dma((nsub, nx, 2, 2)), dma((ny // 2, hx, 2)), dma((nx // 2, hy, 2)),
         dma((ny,)), dma((nx,)), dma(()), dma((ny,)), dma((ny,)), dma((11,)),
     ]
     anyspec = pl.BlockSpec(memory_space=pl.ANY)

time: 89.3 us -> 82.9 us (0.928)
  Pallas kernels: 84.2 us -> 77.8 us
    pallas_call x1, Pallas kernels: 84.2 us -> 77.8 us  [per_device(): pl.pallas_call(functools.partial(kernel, cfg), out_shape=(jax.ShapeDtypeS...]
where the time goes in v4:
time: 82.9 us; the launch traced here: 81.6 us
  Pallas kernels  77.8 us (94%)
  between operations  2.39 us (3%)
  local copies, waits for them, and re-layouts  1.45 us (2%)
    pallas_call x1, Pallas kernels, per_device(): pl.pallas_call(functools.partial(kernel, cfg), out_shape=(jax.ShapeDtypeS...  77.8 us

profile of v4, /device:TPU:516, one launch (start us, length us, event | category | flops | bytes accessed | tf_op | source)
XLA Modules:
  0.0 81.6 jit_solution(7185114173829107933)
XLA Ops:
  0.6 77.8 %routed_experts.1 = (bf16[32,896]{1,0:T(8,128)(2,1)}, s32[1]{0:T(128)}) custom-call(bf16[32,7168]{1,0:T(8,128)(2,1)} %tok_ref.1, bf16[1,7168,256]{2,1,0:T(8,128)(2,1)} %wg_ref.1, bf16[1,7168,256]{2,1,0:T(8,128)(2,1)} %wu_ref.1, bf16[1,256,7168]{2,1,0:T(8,128)(2,1)} %wd_ref.1, f32[8,32]{1,0:T(8,128)} %bitcast.2, s32[8,32]{1,0:T(8,128)} %bitcast.3, s32[4]{0:T(128)} %len_ref.1, ...), custom_call_target="tpu_custom_call" | custom-call | tf_op jit(solution)/shard_map/routed_experts/pallas_call | solution.py:451
  78.4 1.4 %copy.12 = bf16[32,896]{1,0:T(8,128)(2,1)} copy(bf16[32,896]{1,0:T(8,128)(2,1)} %get-tuple-element.4) | data formatting | bytes 114688

commit v5 on v4

--- a/solution.py
+++ b/solution.py
@@ -53,6 +53,35 @@
     return jobs
 
 
+def scatter_jobs(nx, ny, nq, nj, kk, us_unit, us_down):
+    hx, hy = nx // 2, ny // 2
+    pos = {k: p for p, k in enumerate(kk)}
+    jobs = {("down", p): (4, us_down, [("down", p - 1)] if p else [], p) for p in range(ny)}
+    for q in range(nq):
+        for st in range(hx):
+            for d in range(2):
+                deps = [("down", 2 * q + d)] if st == 0 else [("h1", q, st - 1, d), ("down", 2 * q), ("down", 2 * q + 1)]
+                jobs["h1", q, st, d] = (d, us_unit * (1 if st == 0 else 2), deps, 600 + st * 10 + q)
+        for p in (2 * q, 2 * q + 1):
+            if kk[p]:
+                jobs["f1", p] = (2 if kk[p] > 0 else 3, us_unit * abs(kk[p]), [("h1", q, hx - 1, 0), ("h1", q, hx - 1, 1)], 700)
+    for j in range(nj):
+        for st in range(hy):
+            for d in range(2):
+                mine = (j < nj // 2) == (d == 0)
+                if st == 0 and not mine:
+                    continue
+                deps = [("down", pos[hy - st] if (d == 0 or st == 0) else pos[st - hy])]
+                if st > 1 or (st == 1 and mine):
+                    deps.append(("h2", j, st - 1, d))
+                jobs["h2", j, st, d] = (2 + d, us_unit * 2, deps, 600 + st * 10 + j)
+        for slot in (2 * j, 2 * j + 1):
+            if slot:
+                jobs["f2", slot] = (1 if slot <= hx else 0, us_unit * min(slot, nx - slot),
+                                    [("h2", j, hy - 1, 0), ("h2", j, hy - 1, 1), ("down", ny - 1)], 700)
+    return jobs
+
+
 def plan(jobs, lat):
     missing = {k: len(v[2]) for k, v in jobs.items()}
     users = {}
@@ -104,7 +133,8 @@
     partner = {"ep": ep + 1 - 2 * core}
 
     def xdev(d):
-        return {"ep": lax.rem(ep + (2 * d) % n_ep, n_ep)}
+        there = lax.rem(ep + (2 * d) % n_ep, n_ep)
+        return {"ep": there + 1 - 2 * core if d % 2 else there}
 
     def ydev(d):
         return {"tp": lax.rem(tp + d % NY, NY)}
@@ -120,6 +150,11 @@
                                          device_id=dev, device_id_type=MESH)
         c.start()
         return c
+
+    barrier = pltpu.get_barrier_semaphore()
+    peers = [partner, xdev(1), xdev(-1), ydev(1), ydev(-1)]
+    for dev in peers:
+        pl.semaphore_signal(barrier, inc=1, device_id=dev, device_id_type=MESH)
 
     tok_a, tok_b = [], []
     for r in range(NB):
@@ -145,44 +180,40 @@
         c.start()
         dl.append(c)
 
-    barrier = pltpu.get_barrier_semaphore()
-    peers = [partner, xdev(1), xdev(-1), ydev(1), ydev(-1)]
-    for dev in peers:
-        pl.semaphore_signal(barrier, inc=1, device_id=dev, device_id_type=MESH)
-
-    logits = logit_ref[...]
-    sig = 1.0 / (1.0 + jnp.exp(-logits))
-    gates = SCALE * sig / jnp.sum(sig, axis=0, keepdims=True)
-    lane = lax.broadcasted_iota(jnp.int32, (1, rows), 1)
-    length = jnp.zeros((1, rows), jnp.int32)
-    for r in range(rows // DRAFT):
-        length = jnp.where(lane // DRAFT == r, len_ref[r], length)
-    gates = jnp.where(lane % DRAFT < length, gates, 0.0)
-    mrow = lax.broadcasted_iota(jnp.int32, mask_ref.shape, 0)
-    mcol = lax.broadcasted_iota(jnp.int32, mask_ref.shape, 1)
-    mlen = jnp.zeros(mask_ref.shape, jnp.int32)
-    for r in range(rows // DRAFT):
-        mlen = jnp.where(mrow == r, len_ref[r], mlen)
-    passed = jnp.where(mcol < mlen, mask_ref[...], 0).astype(F32)
-    run = passed[:, 0:1]
-    local_count = run
-    for j in range(1, DRAFT):
-        run = run * passed[:, j:j + 1]
-        local_count = local_count + run
-    local_count = jnp.sum(local_count, axis=0, keepdims=True)
-    feat = lax.broadcasted_iota(jnp.int32, (128, rows), 0)
-    dense = jnp.zeros((128, rows), F32)
-    ids = ids_ref[...]
-    for k in range(ids.shape[0]):
-        e = ids[k:k + 1, :]
-        dense = dense + jnp.where((feat == e) | (feat == e + nexp), gates[k:k + 1, :], 0.0)
-    high = dense.astype(BF16)
-    packed = jnp.where(feat < nexp, high.astype(F32), dense - high.astype(F32))
-    packed = packed + jnp.where(feat == 2 * nexp, local_count, 0.0)
-    eye = (lax.broadcasted_iota(jnp.int32, (rows, rows), 0) == lax.broadcasted_iota(jnp.int32, (rows, rows), 1))
-    turned = lax.dot_general(eye.astype(F32).astype(BF16), packed.astype(BF16), (((1,), (1,)), ((), ())),
-                             preferred_element_type=F32)
-    G[0] = turned.astype(BF16)
+    def own_gates():
+        logits = logit_ref[...]
+        sig = 1.0 / (1.0 + jnp.exp(-logits))
+        gates = SCALE * sig / jnp.sum(sig, axis=0, keepdims=True)
+        lane = lax.broadcasted_iota(jnp.int32, (1, rows), 1)
+        length = jnp.zeros((1, rows), jnp.int32)
+        for r in range(rows // DRAFT):
+            length = jnp.where(lane // DRAFT == r, len_ref[r], length)
+        gates = jnp.where(lane % DRAFT < length, gates, 0.0)
+        mrow = lax.broadcasted_iota(jnp.int32, mask_ref.shape, 0)
+        mcol = lax.broadcasted_iota(jnp.int32, mask_ref.shape, 1)
+        mlen = jnp.zeros(mask_ref.shape, jnp.int32)
+        for r in range(rows // DRAFT):
+            mlen = jnp.where(mrow == r, len_ref[r], mlen)
+        passed = jnp.where(mcol < mlen, mask_ref[...], 0).astype(F32)
+        run = passed[:, 0:1]
+        local_count = run
+        for j in range(1, DRAFT):
+            run = run * passed[:, j:j + 1]
+            local_count = local_count + run
+        local_count = jnp.sum(local_count, axis=0, keepdims=True)
+        feat = lax.broadcasted_iota(jnp.int32, (128, rows), 0)
+        dense = jnp.zeros((128, rows), F32)
+        ids = ids_ref[...]
+        for k in range(ids.shape[0]):
+            e = ids[k:k + 1, :]
+            dense = dense + jnp.where((feat == e) | (feat == e + nexp), gates[k:k + 1, :], 0.0)
+        high = dense.astype(BF16)
+        packed = jnp.where(feat < nexp, high.astype(F32), dense - high.astype(F32))
+        packed = packed + jnp.where(feat == 2 * nexp, local_count, 0.0)
+        eye = (lax.broadcasted_iota(jnp.int32, (rows, rows), 0) == lax.broadcasted_iota(jnp.int32, (rows, rows), 1))
+        turned = lax.dot_general(eye.astype(F32).astype(BF16), packed.astype(BF16), (((1,), (1,)), ((), ())),
+                                 preferred_element_type=F32)
+        G[0] = turned.astype(BF16)
 
     pl.semaphore_wait(barrier, len(peers))
 
@@ -224,6 +255,9 @@
             own_ready("b", 0)
             src, dst, sem, recv = XB.at[0, a, take, cols], XB.at[0, b, take, cols], B_SEND, b_recv.at[n, st, d]
         else:
+            if "gates" not in heard:
+                heard.add("gates")
+                own_gates()
             src, dst, sem, recv = G.at[a, take], G.at[b, take], G_SEND, g_recv.at[st, d]
         copies[key] = remote(src, dst, sem, recv, xdev(1 if d == 0 else -1))
 
@@ -301,85 +335,79 @@
         P2[p] = y[:, half:]
 
     pos = {k: p for p, k in enumerate(kk)}
-    NQ = NY // 2
-    NJ = NX // 2
-    h1, h2 = {}, {}
-
-    def add(dst, src):
-        dst[...] = (dst[...].astype(F32) + src[...].astype(F32)).astype(BF16)
-
-    def h1_step(q, s):
-        for d in range(2):
-            slot = (HX + s) % NX if d == 0 else HX - s
-            if s == 0:
-                p, n = 2 * q + d, 1
-            else:
-                p, n = 2 * q, 2
-                h1[q, s - 1, d].wait_recv()
-                pa, na = (2 * q + d, 1) if s == 1 else (p, n)
-                add(P1.at[pl.ds(pa, na), slot], RB1.at[d, s - 1, pl.ds(pa, na)])
-            h1[q, s, d] = remote(P1.at[pl.ds(p, n), slot], RB1.at[d, s, pl.ds(p, n)],
-                                 H1_SEND, h1_recv.at[q, s, d], xdev(1 if d == 0 else -1))
-
-    def h2_step(j, s):
-        for d in range(2):
-            p = pos[HY - s] if (d == 0 or s == 0) else pos[s - HY]
-            mine = (j < NJ // 2) == (d == 0)
-            rng = pl.ds(2 * j, 2)
-            if s == 0 and not mine:
-                continue
-            if s > 0 and (s > 1 or mine):
-                h2[j, s - 1, d].wait_recv()
-                add(P2.at[p, rng], RB2.at[d, s - 1, rng])
-            h2[j, s, d] = remote(P2.at[p, rng], RB2.at[d, s, rng],
-                                 H2_SEND, h2_recv.at[j, s, d], ydev(1 if d == 0 else -1))
-
-    down(0)
+    NQ, NJ = NY // 2, NX // 2
+    last = NY - 1
+    jobs2 = scatter_jobs(NX, NY, NQ, NJ, kk, cfg["us_unit"], cfg["us_down"])
+    sent = {}
+    done = set()
+
+    def once(key):
+        if key in done:
+            return False
+        done.add(key)
+        return True
+
+    def add(dst, *srcs):
+        total = dst[...].astype(F32)
+        for src in srcs:
+            total = total + src[...].astype(F32)
+        dst[...] = total.astype(BF16)
+
+    def h1_step(q, s, d):
+        slot = (HX + s) % NX if d == 0 else HX - s
+        if s == 0:
+            p, n = 2 * q + d, 1
+        else:
+            p, n = 2 * q, 2
+            sent["h1", q, s - 1, d].wait_recv()
+            pa, na = (2 * q + d, 1) if s == 1 else (p, n)
+            add(P1.at[pl.ds(pa, na), slot], RB1.at[d, s - 1, pl.ds(pa, na)])
+        sent["h1", q, s, d] = remote(P1.at[pl.ds(p, n), slot], RB1.at[d, s, pl.ds(p, n)], H1_SEND, h1_recv.at[q, s, d],
+                                     xdev(1 if d == 0 else -1))
+
+    def h2_step(j, s, d):
+        p = pos[HY - s] if (d == 0 or s == 0) else pos[s - HY]
+        rng = pl.ds(2 * j, 2)
+        if ("h2", j, s - 1, d) in sent:
+            sent["h2", j, s - 1, d].wait_recv()
+            add(P2.at[p, rng], RB2.at[d, s - 1, rng])
+        sent["h2", j, s, d] = remote(P2.at[p, rng], RB2.at[d, s, rng], H2_SEND, h2_recv.at[j, s, d], ydev(1 if d == 0 else -1))
+
+    def h1_final(q):
+        if once(("h1", q)):
+            sent["h1", q, HX - 1, 0].wait_recv()
+            sent["h1", q, HX - 1, 1].wait_recv()
+            r = pl.ds(2 * q, 2)
+            add(P1.at[r, 0], RB1.at[0, HX - 1, r], RB1.at[1, HX - 1, r])
+
+    def h2_final(j):
+        if once(("h2", j)):
+            sent["h2", j, HY - 1, 0].wait_recv()
+            sent["h2", j, HY - 1, 1].wait_recv()
+            r = pl.ds(2 * j, 2)
+            add(P2.at[last, r], RB2.at[0, HY - 1, r], RB2.at[1, HY - 1, r])
+
+    f1, f2 = [], []
+    for _, key in plan(jobs2, cfg["lat2"]):
+        if key[0] == "down":
+            down(key[1])
+        elif key[0] == "h1":
+            h1_step(*key[1:])
+        elif key[0] == "h2":
+            h2_step(*key[1:])
+        elif key[0] == "f1":
+            p = key[1]
+            h1_final(p // 2)
+            f1.append(remote(P1.at[p, 0], F1.at[p], F1_SEND, f1_recv.at[p], ydev(kk[p])))
+        else:
+            slot = key[1]
+            h2_final(slot // 2)
+            f2.append(remote(P2.at[last, slot], F2.at[slot], F2_SEND, f2_recv.at[slot], xdev(-slot)))
+
+    for q in range(NQ):
+        h1_final(q)
     for j in range(NJ):
-        h2_step(j, 0)
-    down(1)
-    h1_step(0, 0)
-    for q in range(1, NQ):
-        down(2 * q)
-        down(2 * q + 1)
-        h1_step(q, 0)
-        if q == 1:
-            for j in range(NJ):
-                h2_step(j, 1)
-    for s in range(1, HX):
-        for i in range(max(NQ, NJ)):
-            if i < NQ:
-                h1_step(i, s)
-            if i < NJ and s + 1 < HY:
-                h2_step(i, s + 1)
-
-    f1, f2 = [], []
-    last = NY - 1
-
-    def h1_final(q):
-        h1[q, HX - 1, 0].wait_recv()
-        h1[q, HX - 1, 1].wait_recv()
-        r = pl.ds(2 * q, 2)
-        P1[r, 0] = (P1[r, 0].astype(F32) + RB1[0, HX - 1, r].astype(F32) + RB1[1, HX - 1, r].astype(F32)).astype(BF16)
-        for p in (2 * q, 2 * q + 1):
-            if kk[p] != 0:
-                f1.append(remote(P1.at[p, 0], F1.at[p], F1_SEND, f1_recv.at[p], ydev(kk[p])))
-
-    def h2_final(j):
-        h2[j, HY - 1, 0].wait_recv()
-        h2[j, HY - 1, 1].wait_recv()
-        r = pl.ds(2 * j, 2)
-        P2[last, r] = (P2[last, r].astype(F32) + RB2[0, HY - 1, r].astype(F32) + RB2[1, HY - 1, r].astype(F32)).astype(BF16)
-        for slot in (2 * j, 2 * j + 1):
-            if slot != 0:
-                f2.append(remote(P2.at[last, slot], F2.at[slot], F2_SEND, f2_recv.at[slot], xdev(-slot)))
-
-    for i in range(max(NQ, NJ)):
-        if i < NJ:
-            h2_final(i)
-        if i < NQ:
-            h1_final(i)
-
+        h2_final(j)
     for c in f1 + f2:
         c.wait_recv()
     a = P1[last, 0].astype(F32)
@@ -425,7 +453,8 @@
     ka = (width - nb * kb) // na
     us_per_col = rows * 2 / 46.6e3
     cfg = dict(nx=nx, ny=ny, na=na, ka=ka, nb=nb, nsub=nsub, kb=kb, rows=rows, ncol=ncol, hid=hid,
-               nexp=lax.axis_size("ep"), us_per_col=us_per_col, us_dot=0.6e-3, lat=3.2, push_rate=450e3)
+               nexp=lax.axis_size("ep"), us_per_col=us_per_col, us_dot=0.6e-3, lat=3.2, push_rate=450e3,
+               us_unit=half * ncol * 2 / 46.6e3, us_down=0.27, lat2=3.5)
     dma = pltpu.SemaphoreType.DMA
     scratch = [
         pltpu.VMEM((na, nx, rows, ka), BF16),

time: 82.9 us -> 79.2 us (0.955)
  Pallas kernels: 77.8 us -> 74.6 us
    pallas_call x1, Pallas kernels: 77.8 us -> 74.6 us  [per_device(): pl.pallas_call(functools.partial(kernel, cfg), out_shape=(jax.ShapeDtypeS...]
where the time goes in v5:
time: 79.2 us; the launch traced here: 78.5 us
  Pallas kernels  74.6 us (94%)
  between operations  2.39 us (3%)
  local copies, waits for them, and re-layouts  1.45 us (2%)
    pallas_call x1, Pallas kernels, per_device(): pl.pallas_call(functools.partial(kernel, cfg), out_shape=(jax.ShapeDtypeS...  74.6 us

profile of v5, /device:TPU:516, one launch (start us, length us, event | category | flops | bytes accessed | tf_op | source)
XLA Modules:
  0.0 78.5 jit_solution(1047991694970984556)
XLA Ops:
  0.6 74.6 %routed_experts.1 = (bf16[32,896]{1,0:T(8,128)(2,1)}, s32[1]{0:T(128)}) custom-call(bf16[32,7168]{1,0:T(8,128)(2,1)} %tok_ref.1, bf16[1,7168,256]{2,1,0:T(8,128)(2,1)} %wg_ref.1, bf16[1,7168,256]{2,1,0:T(8,128)(2,1)} %wu_ref.1, bf16[1,256,7168]{2,1,0:T(8,128)(2,1)} %wd_ref.1, f32[8,32]{1,0:T(8,128)} %bitcast.2, s32[8,32]{1,0:T(8,128)} %bitcast.3, s32[4]{0:T(128)} %len_ref.1, ...), custom_call_target="tpu_custom_call" | custom-call | tf_op jit(solution)/shard_map/routed_experts/pallas_call | solution.py:480
  75.3 1.4 %copy.12 = bf16[32,896]{1,0:T(8,128)(2,1)} copy(bf16[32,896]{1,0:T(8,128)(2,1)} %get-tuple-element.4) | data formatting | bytes 114688

commit v6 on v5

--- a/solution.py
+++ b/solution.py
@@ -62,9 +62,16 @@
             for d in range(2):
                 deps = [("down", 2 * q + d)] if st == 0 else [("h1", q, st - 1, d), ("down", 2 * q), ("down", 2 * q + 1)]
                 jobs["h1", q, st, d] = (d, us_unit * (1 if st == 0 else 2), deps, 600 + st * 10 + q)
+        ready = [("h1", q, hx - 1, 0), ("h1", q, hx - 1, 1)]
         for p in (2 * q, 2 * q + 1):
-            if kk[p]:
-                jobs["f1", p] = (2 if kk[p] > 0 else 3, us_unit * abs(kk[p]), [("h1", q, hx - 1, 0), ("h1", q, hx - 1, 1)], 700)
+            far = abs(kk[p])
+            if far == hy:
+                for d in range(2):
+                    jobs["e1", d] = (2 + d, us_unit / 2, ready, 500)
+            elif far:
+                relay = [("e1", 0 if kk[p] > 0 else 1)] if far == hy - 1 else []
+                jobs["f1", p] = (2 if kk[p] > 0 else 3, us_unit * far, ready + relay, 700 - far)
+    by_distance = sorted(range(nj), key=lambda j: (-max(min(m, nx - m) for m in (2 * j, 2 * j + 1)), j))
     for j in range(nj):
         for st in range(hy):
             for d in range(2):
@@ -74,11 +81,16 @@
                 deps = [("down", pos[hy - st] if (d == 0 or st == 0) else pos[st - hy])]
                 if st > 1 or (st == 1 and mine):
                     deps.append(("h2", j, st - 1, d))
-                jobs["h2", j, st, d] = (2 + d, us_unit * 2, deps, 600 + st * 10 + j)
+                jobs["h2", j, st, d] = (2 + d, us_unit * 2, deps, 600 + st * 10 + by_distance.index(j))
+        ready = [("h2", j, hy - 1, 0), ("h2", j, hy - 1, 1), ("down", ny - 1)]
         for slot in (2 * j, 2 * j + 1):
-            if slot:
-                jobs["f2", slot] = (1 if slot <= hx else 0, us_unit * min(slot, nx - slot),
-                                    [("h2", j, hy - 1, 0), ("h2", j, hy - 1, 1), ("down", ny - 1)], 700)
+            far = min(slot, nx - slot)
+            if far == hx:
+                for d in range(2):
+                    jobs["e2", d] = (1 - d, us_unit / 2, ready, 500)
+            elif far:
+                relay = [("e2", 0 if slot < hx else 1)] if far == hx - 1 else []
+                jobs["f2", slot] = (1 if slot < hx else 0, us_unit * far, ready + relay, 700 - far)
     return jobs
 
 
@@ -114,9 +126,9 @@
 
 
 def kernel(cfg, tok_ref, wg_ref, wu_ref, wd_ref, logit_ref, ids_ref, len_ref, mask_ref, out_ref, count_ref,
-           XA, XB, G, W, WD, ACC, P1, P2, RB1, RB2, F1, F2, C,
+           XA, XB, G, W, WD, ACC, P1, P2, RB1, RB2, F1, F2, E, O, C,
            ta_sem, tb_sem, wla_sem, wlb_sem, wra_sem, wrb_sem, a_recv, b_recv, g_recv, y_recv, h1_recv, h2_recv,
-           f1_recv, f2_recv, c_recv, d_sem, dr_recv, send_sem):
+           f1_recv, f2_recv, e_recv, out_sem, c_recv, d_sem, dr_recv, send_sem):
     NX, NY, NA, NB, NSUB = cfg["nx"], cfg["ny"], cfg["na"], cfg["nb"], cfg["nsub"]
     HX, HY = NX // 2, NY // 2
     rows = cfg["rows"]
@@ -143,7 +155,7 @@
         return pl.ds(pl.multiple_of(start + lax.rem(tp + r % count, count) * size, 128), size)
 
     kk = signed_order(NY)
-    A_SEND, B_SEND, G_SEND, Y_SEND, H1_SEND, H2_SEND, F1_SEND, F2_SEND, C_SEND, W_SEND, D_SEND = range(11)
+    A_SEND, B_SEND, G_SEND, Y_SEND, H1_SEND, H2_SEND, F1_SEND, F2_SEND, C_SEND, W_SEND, D_SEND, E_SEND = range(12)
 
     def remote(src, dst, send, recv, dev):
         c = pltpu.make_async_remote_copy(src_ref=src, dst_ref=dst, send_sem=send_sem.at[send], recv_sem=recv,
@@ -388,6 +400,8 @@
             add(P2.at[last, r], RB2.at[0, HY - 1, r], RB2.at[1, HY - 1, r])
 
     f1, f2 = [], []
+    cut = -(-(ncol // 128) // 2) * 128
+    parts = (pl.ds(0, cut), pl.ds(cut, ncol - cut))
     for _, key in plan(jobs2, cfg["lat2"]):
         if key[0] == "down":
             down(key[1])
@@ -395,30 +409,47 @@
             h1_step(*key[1:])
         elif key[0] == "h2":
             h2_step(*key[1:])
+        elif key[0] == "e1":
+            d = key[1]
+            h1_final(pos[HY] // 2)
+            sent[key] = remote(P1.at[pos[HY], 0, :, parts[d]], E.at[0, :, parts[d]], E_SEND, e_recv.at[0, d],
+                               ydev(1 if d == 0 else -1))
+        elif key[0] == "e2":
+            d = key[1]
+            h2_final(HX // 2)
+            sent[key] = remote(P2.at[last, HX, :, parts[d]], E.at[1, :, parts[d]], E_SEND, e_recv.at[1, d],
+                               xdev(-1 if d == 0 else 1))
         elif key[0] == "f1":
             p = key[1]
             h1_final(p // 2)
-            f1.append(remote(P1.at[p, 0], F1.at[p], F1_SEND, f1_recv.at[p], ydev(kk[p])))
+            if abs(kk[p]) == HY - 1:
+                d = 0 if kk[p] > 0 else 1
+                sent["e1", d].wait_recv()
+                add(P1.at[p, 0, :, parts[d]], E.at[0, :, parts[d]])
+            f1.append((p, remote(P1.at[p, 0], F1.at[p], F1_SEND, f1_recv.at[p], ydev(kk[p]))))
         else:
             slot = key[1]
             h2_final(slot // 2)
-            f2.append(remote(P2.at[last, slot], F2.at[slot], F2_SEND, f2_recv.at[slot], xdev(-slot)))
+            if min(slot, NX - slot) == HX - 1:
+                d = 0 if slot < HX else 1
+                sent["e2", d].wait_recv()
+                add(P2.at[last, slot, :, parts[d]], E.at[1, :, parts[d]])
+            f2.append((slot, remote(P2.at[last, slot], F2.at[slot], F2_SEND, f2_recv.at[slot], xdev(-slot))))
 
     for q in range(NQ):
         h1_final(q)
     for j in range(NJ):
         h2_final(j)
-    for c in f1 + f2:
-        c.wait_recv()
-    a = P1[last, 0].astype(F32)
-    for p in range(NY):
-        if kk[p] != 0:
-            a = a + F1[p].astype(F32)
-    out_ref[pl.ds(0, half), :] = a.astype(BF16)
-    b = P2[last, 0].astype(F32)
-    for slot in range(1, NX):
-        b = b + F2[slot].astype(F32)
-    out_ref[pl.ds(half, half), :] = b.astype(BF16)
+    out_copies = []
+    for n, (own, arrived, ref) in enumerate(((P1.at[last, 0], f1, F1), (P2.at[last, 0], f2, F2))):
+        total = own[...].astype(F32)
+        for m, c in arrived:
+            c.wait_recv()
+            total = total + ref[m].astype(F32)
+        O[n] = total.astype(BF16)
+        c = pltpu.make_async_copy(O.at[n], out_ref.at[pl.ds(n * half, half)], out_sem.at[n])
+        c.start()
+        out_copies.append(c)
     c_copy.wait_recv()
     first_only = ((lax.broadcasted_iota(jnp.int32, (8, 128), 0) == 0)
                   & (lax.broadcasted_iota(jnp.int32, (8, 128), 1) == 0))
@@ -437,8 +468,11 @@
     drained(C_SEND, C.at[0])
     drained(H1_SEND, P1.at[:, most])
     drained(H2_SEND, P2.at[pl.ds(0, NY - 1)])
-    drained(F1_SEND, F1.at[pl.ds(0, NY - 1)])
-    drained(F2_SEND, F2.at[most])
+    drained(E_SEND, E)
+    drained(F1_SEND, F1.at[pl.ds(0, NY - 2)])
+    drained(F2_SEND, F2.at[pl.ds(0, NX - 2)])
+    for c in out_copies:
+        c.wait()
 
 
 def per_device(tokens, w_gate, w_up, w_down, router_logits, expert_ids, draft_lengths, accept_mask):
@@ -454,7 +488,7 @@
     us_per_col = rows * 2 / 46.6e3
     cfg = dict(nx=nx, ny=ny, na=na, ka=ka, nb=nb, nsub=nsub, kb=kb, rows=rows, ncol=ncol, hid=hid,
                nexp=lax.axis_size("ep"), us_per_col=us_per_col, us_dot=0.6e-3, lat=3.2, push_rate=450e3,
-               us_unit=half * ncol * 2 / 46.6e3, us_down=0.27, lat2=3.5)
+               us_unit=half * ncol * 2 / 46.6e3, us_down=0.27, lat2=2.4)
     dma = pltpu.SemaphoreType.DMA
     scratch = [
         pltpu.VMEM((na, nx, rows, ka), BF16),
@@ -469,10 +503,12 @@
         pltpu.VMEM((2, hy, nx, half, ncol), BF16),
         pltpu.VMEM((ny, half, ncol), BF16),
         pltpu.VMEM((nx, half, ncol), BF16),
+        pltpu.VMEM((2, half, ncol), BF16),
+        pltpu.VMEM((2, half, ncol), BF16),
         pltpu.VMEM((2, 8, 128), F32),
         dma((na,)), dma((nb,)), dma((na,)), dma((nb,)), dma((na,)), dma((nb,)),
         dma((na, hx, 2)), dma((nsub, hx, 2)), dma((hx, 2)), dma((nsub, nx, 2, 2)), dma((ny // 2, hx, 2)), dma((nx // 2, hy, 2)),
-        dma((ny,)), dma((nx,)), dma(()), dma((ny,)), dma((ny,)), dma((11,)),
+        dma((ny,)), dma((nx,)), dma((2, 2)), dma((2,)), dma(()), dma((ny,)), dma((ny,)), dma((12,)),
     ]
     anyspec = pl.BlockSpec(memory_space=pl.ANY)
     vmem = pl.BlockSpec(memory_space=pltpu.VMEM)
@@ -481,7 +517,7 @@
         functools.partial(kernel, cfg),
         out_shape=(jax.ShapeDtypeStruct((rows, ncol), BF16), jax.ShapeDtypeStruct((1,), jnp.int32)),
         in_specs=[anyspec] * 4 + [vmem, vmem, smem, vmem],
-        out_specs=(vmem, smem),
+        out_specs=(anyspec, smem),
         scratch_shapes=scratch,
         name="routed_experts",
         compiler_params=pltpu.CompilerParams(collective_id=0, has_side_effects=True, vmem_limit_bytes=60 * 1024 * 1024),

time: 79.2 us -> 78.6 us (level)
  no operation moved by 1% of the time
where the time goes in v6:
time: 78.6 us; the launch traced here: 77.9 us
  Pallas kernels  74.1 us (94%)
  between operations  2.39 us (3%)
  local copies, waits for them, and re-layouts  1.45 us (2%)
    pallas_call x1, Pallas kernels, per_device(): pl.pallas_call(functools.partial(kernel, cfg), out_shape=(jax.ShapeDtypeS...  74.1 us

profile of v6, /device:TPU:516, one launch (start us, length us, event | category | flops | bytes accessed | tf_op | source)
XLA Modules:
  0.0 77.9 jit_solution(11511912158097892986)
XLA Ops:
  0.6 74.1 %routed_experts.1 = (bf16[32,896]{1,0:T(8,128)(2,1)}, s32[1]{0:T(128)}) custom-call(bf16[32,7168]{1,0:T(8,128)(2,1)} %tok_ref.1, bf16[1,7168,256]{2,1,0:T(8,128)(2,1)} %wg_ref.1, bf16[1,7168,256]{2,1,0:T(8,128)(2,1)} %wu_ref.1, bf16[1,256,7168]{2,1,0:T(8,128)(2,1)} %wd_ref.1, f32[8,32]{1,0:T(8,128)} %bitcast.2, s32[8,32]{1,0:T(8,128)} %bitcast.3, s32[4]{0:T(128)} %len_ref.1, ...), custom_call_target="tpu_custom_call" | custom-call | tf_op jit(solution)/shard_map/routed_experts/pallas_call | solution.py:516
  74.7 1.4 %copy.12 = bf16[32,896]{1,0:T(8,128)(2,1)} copy(bf16[32,896]{1,0:T(8,128)(2,1)} %get-tuple-element.4) | data formatting | bytes 114688

commit v7 on v6

--- a/solution.py
+++ b/solution.py
@@ -126,9 +126,9 @@
 
 
 def kernel(cfg, tok_ref, wg_ref, wu_ref, wd_ref, logit_ref, ids_ref, len_ref, mask_ref, out_ref, count_ref,
-           XA, XB, G, W, WD, ACC, P1, P2, RB1, RB2, F1, F2, E, O, C,
+           XA, XB, G, W, WD, ACC, P1, P2, RB1, RB2, F1, F2, E, C,
            ta_sem, tb_sem, wla_sem, wlb_sem, wra_sem, wrb_sem, a_recv, b_recv, g_recv, y_recv, h1_recv, h2_recv,
-           f1_recv, f2_recv, e_recv, out_sem, c_recv, d_sem, dr_recv, send_sem):
+           f1_recv, f2_recv, e_recv, c_recv, d_sem, dr_recv, send_sem):
     NX, NY, NA, NB, NSUB = cfg["nx"], cfg["ny"], cfg["na"], cfg["nb"], cfg["nsub"]
     HX, HY = NX // 2, NY // 2
     rows = cfg["rows"]
@@ -440,16 +440,12 @@
         h1_final(q)
     for j in range(NJ):
         h2_final(j)
-    out_copies = []
     for n, (own, arrived, ref) in enumerate(((P1.at[last, 0], f1, F1), (P2.at[last, 0], f2, F2))):
         total = own[...].astype(F32)
         for m, c in arrived:
             c.wait_recv()
             total = total + ref[m].astype(F32)
-        O[n] = total.astype(BF16)
-        c = pltpu.make_async_copy(O.at[n], out_ref.at[pl.ds(n * half, half)], out_sem.at[n])
-        c.start()
-        out_copies.append(c)
+        out_ref[pl.ds(n * half, half), :] = total.astype(BF16)
     c_copy.wait_recv()
     first_only = ((lax.broadcasted_iota(jnp.int32, (8, 128), 0) == 0)
                   & (lax.broadcasted_iota(jnp.int32, (8, 128), 1) == 0))
@@ -471,8 +467,6 @@
     drained(E_SEND, E)
     drained(F1_SEND, F1.at[pl.ds(0, NY - 2)])
     drained(F2_SEND, F2.at[pl.ds(0, NX - 2)])
-    for c in out_copies:
-        c.wait()
 
 
 def per_device(tokens, w_gate, w_up, w_down, router_logits, expert_ids, draft_lengths, accept_mask):
@@ -487,7 +481,7 @@
     ka = (width - nb * kb) // na
     us_per_col = rows * 2 / 46.6e3
     cfg = dict(nx=nx, ny=ny, na=na, ka=ka, nb=nb, nsub=nsub, kb=kb, rows=rows, ncol=ncol, hid=hid,
-               nexp=lax.axis_size("ep"), us_per_col=us_per_col, us_dot=0.6e-3, lat=3.2, push_rate=450e3,
+               nexp=lax.axis_size("ep"), us_per_col=us_per_col, us_dot=0.6e-3, lat=3.0, push_rate=450e3,
                us_unit=half * ncol * 2 / 46.6e3, us_down=0.27, lat2=2.4)
     dma = pltpu.SemaphoreType.DMA
     scratch = [
@@ -504,20 +498,19 @@
         pltpu.VMEM((ny, half, ncol), BF16),
         pltpu.VMEM((nx, half, ncol), BF16),
         pltpu.VMEM((2, half, ncol), BF16),
-        pltpu.VMEM((2, half, ncol), BF16),
         pltpu.VMEM((2, 8, 128), F32),
         dma((na,)), dma((nb,)), dma((na,)), dma((nb,)), dma((na,)), dma((nb,)),
         dma((na, hx, 2)), dma((nsub, hx, 2)), dma((hx, 2)), dma((nsub, nx, 2, 2)), dma((ny // 2, hx, 2)), dma((nx // 2, hy, 2)),
-        dma((ny,)), dma((nx,)), dma((2, 2)), dma((2,)), dma(()), dma((ny,)), dma((ny,)), dma((12,)),
+        dma((ny,)), dma((nx,)), dma((2, 2)), dma(()), dma((ny,)), dma((ny,)), dma((12,)),
     ]
     anyspec = pl.BlockSpec(memory_space=pl.ANY)
     vmem = pl.BlockSpec(memory_space=pltpu.VMEM)
     smem = pl.BlockSpec(memory_space=pltpu.SMEM)
     mixed, accepted = pl.pallas_call(
         functools.partial(kernel, cfg),
-        out_shape=(jax.ShapeDtypeStruct((rows, ncol), BF16), jax.ShapeDtypeStruct((1,), jnp.int32)),
+        out_shape=(pltpu.VMEM((rows, ncol), BF16), jax.ShapeDtypeStruct((1,), jnp.int32)),
         in_specs=[anyspec] * 4 + [vmem, vmem, smem, vmem],
-        out_specs=(anyspec, smem),
+        out_specs=(vmem, smem),
         scratch_shapes=scratch,
         name="routed_experts",
         compiler_params=pltpu.CompilerParams(collective_id=0, has_side_effects=True, vmem_limit_bytes=60 * 1024 * 1024),

time: 78.6 us -> 77.7 us (0.989)
  local copies, waits for them, and re-layouts: 1.45 us -> 0.63 us
    unnamed x1, local copies, waits for them, and re-layouts: 1.45 us -> 0.63 us
where the time goes in v7:
time: 77.7 us; the launch traced here: 77.5 us
  Pallas kernels  74.6 us (96%)
  between operations  2.33 us (3%)
    pallas_call x1, Pallas kernels, per_device(): pl.pallas_call(functools.partial(kernel, cfg), out_shape=(pltpu.VMEM((row...  74.6 us

profile of v7, /device:TPU:516, one launch (start us, length us, event | category | flops | bytes accessed | tf_op | source)
XLA Modules:
  0.0 77.5 jit_solution(17624104838076222032)
XLA Ops:
  0.6 74.6 %routed_experts.1 = (bf16[32,896]{1,0:T(8,128)(2,1)S(1)}, s32[1]{0:T(128)}) custom-call(bf16[32,7168]{1,0:T(8,128)(2,1)} %tok_ref.1, bf16[1,7168,256]{2,1,0:T(8,128)(2,1)} %wg_ref.1, bf16[1,7168,256]{2,1,0:T(8,128)(2,1)} %wu_ref.1, bf16[1,256,7168]{2,1,0:T(8,128)(2,1)} %wd_ref.1, f32[8,32]{1,0:T(8,128)} %bitcast.2, s32[8,32]{1,0:T(8,128)} %bitcast.3, ...), custom_call_target="tpu_custom_call" | custom-call | tf_op jit(solution)/shard_map/routed_experts/pallas_call | solution.py:509
  75.2 0.6 copy.12

commit v8 on v7

--- a/solution.py
+++ b/solution.py
@@ -476,12 +476,12 @@
     ncol = width // ny
     half = rows // 2
     hx, hy = nx // 2, ny // 2
-    nb, nsub, kb = 4, 2, 1024
-    na = 3
+    nb, nsub, kb = 4, 3, 1152
+    na = 2
     ka = (width - nb * kb) // na
     us_per_col = rows * 2 / 46.6e3
     cfg = dict(nx=nx, ny=ny, na=na, ka=ka, nb=nb, nsub=nsub, kb=kb, rows=rows, ncol=ncol, hid=hid,
-               nexp=lax.axis_size("ep"), us_per_col=us_per_col, us_dot=0.6e-3, lat=3.0, push_rate=450e3,
+               nexp=lax.axis_size("ep"), us_per_col=us_per_col, us_dot=0.6e-3, lat=2.8, push_rate=450e3,
                us_unit=half * ncol * 2 / 46.6e3, us_down=0.27, lat2=2.4)
     dma = pltpu.SemaphoreType.DMA
     scratch = [

time: 77.7 us -> 78.2 us (level)
  no operation moved by 1% of the time
where the time goes in v8:
time: 78.2 us; the launch traced here: 77.9 us
  Pallas kernels  74.9 us (96%)
  between operations  2.33 us (3%)
    pallas_call x1, Pallas kernels, per_device(): pl.pallas_call(functools.partial(kernel, cfg), out_shape=(pltpu.VMEM((row...  74.9 us

profile of v8, /device:TPU:516, one launch (start us, length us, event | category | flops | bytes accessed | tf_op | source)
XLA Modules:
  0.0 77.9 jit_solution(11752696499548300051)
XLA Ops:
  0.6 74.9 %routed_experts.1 = (bf16[32,896]{1,0:T(8,128)(2,1)S(1)}, s32[1]{0:T(128)}) custom-call(bf16[32,7168]{1,0:T(8,128)(2,1)} %tok_ref.1, bf16[1,7168,256]{2,1,0:T(8,128)(2,1)} %wg_ref.1, bf16[1,7168,256]{2,1,0:T(8,128)(2,1)} %wu_ref.1, bf16[1,256,7168]{2,1,0:T(8,128)(2,1)} %wd_ref.1, f32[8,32]{1,0:T(8,128)} %bitcast.2, s32[8,32]{1,0:T(8,128)} %bitcast.3, ...), custom_call_target="tpu_custom_call" | custom-call | tf_op jit(solution)/shard_map/routed_experts/pallas_call | solution.py:509
  75.6 0.6 copy.12
